TPU v7x, 32 devices: a whole 2x2x4 slice. The times are simulated.
32 devices in a mesh: groups: 1, role: 2 (over core), dev: 16 (over z, y, x).
Axes of the slice: x: 2, y: 2, z: 4, core: 2. Of those that a mesh axis runs over, the one named last changes fastest.
Arguments:
- prompt_hidden: bfloat16 [4096, 4096], P(('groups', 'dev')), may hold values from -6 to 6
- norm_gain: float32 [4096], replicated, may hold values from 0.25 to 1.75
- kv_weight: bfloat16 [4096, 4, 2, 128], P(None, 'role'), may hold values from -0.09375 to 0.09375
- prompt_excess: int32 [4], P('groups'), may hold values from 1 to 1536, 2048 in all
- prompt_owner: int32 [4], P('groups'), may hold values from 0 to 15, as said below
- response_counts: int32 [4], P('groups'), may hold values from 1 to 5, as said below
- queries: bfloat16 [256, 16, 128], P(('groups', 'dev'), 'role'), may hold values from -256 to 256
- new_kv: bfloat16 [256, 4, 2, 128], P(('groups', 'dev'), 'role'), may hold values from -6 to 6
- response_cache: bfloat16 [256, 256, 4, 2, 128], P(('groups', 'dev'), None, 'role'), may hold values from -6 to 6
- positions: int32 [256], P(('groups', 'dev')), may hold values from 0 to 256
- out_weight: bfloat16 [16, 128, 4096], P('role', None, 'dev'), may hold values from -0.125 to 0.125
Outputs:
- attended: bfloat16 [256, 16, 128], P(('groups', 'dev'), 'role')
- block_out: bfloat16 [256, 4096], P(('groups', 'role'), 'dev')
Inputs may be any that keep to these rules, and one draw needn't show every extreme that they name: `prompt_owner`: no device along dev owns more than two prompts, and some device owns exactly two. `response_counts`: some prompt has exactly 5 responses.
All inputs are finite; a program needn't handle non-finite values.
Results may differ from a plain program's by a relative error of at most 0.0065.
Values may be sent and summed in bfloat16 or wider, within the bound.
No kernel may reach another device: no remote copies, remote signals or barrier semaphores. Data moves between devices by JAX's collectives and lax.ppermute only.
A program may use at most 192 MiB of HBM per device.

v0:
```python
import jax
import jax.numpy as jnp
from jax import lax
from jax.sharding import PartitionSpec as P

RESP = 5
PROMPT_MIN = 512


rope_base = 500000.0


def merged_2(part, axis, combine):
    gathered = jax.tree.map(lambda a: lax.all_gather(a, axis), part)

    def take(source):
        return jax.tree.map(lambda a: lax.dynamic_index_in_dim(a, source, 0, False), gathered)

    return lax.fori_loop(
        1, lax.axis_size(axis), lambda source, state: combine(state, take(source)), take(0)
    )


def rotate(vectors, offsets):
    half = vectors.shape[-1] // 2
    freq = rope_base ** (-jnp.arange(half, dtype=jnp.float32) * 2.0 / vectors.shape[-1])
    angles = offsets.astype(jnp.float32)[:, None] * freq[None, :]
    cosine = jnp.cos(angles)[:, None, :]
    sine = jnp.sin(angles)[:, None, :]
    first = vectors[..., :half]
    second = vectors[..., half:]
    return jnp.concatenate(
        [first * cosine - second * sine, second * cosine + first * sine], axis=-1
    )


def prompt_layout(prompt_excess, token_index):
    lengths = PROMPT_MIN + prompt_excess
    ends = jnp.cumsum(lengths)
    starts = ends - lengths
    prompt_id = jnp.sum((token_index[:, None] >= ends[None, :]).astype(jnp.int32), axis=1)
    member = prompt_id[:, None] == jnp.arange(lengths.shape[0], dtype=jnp.int32)[None, :]
    offsets = token_index - jnp.sum(jnp.where(member, starts[None, :], 0), axis=1)
    return (member, offsets, starts, lengths)


def first_slots(owner, counts):
    order = jnp.arange(owner.shape[0], dtype=jnp.int32)
    earlier = (owner[:, None] == owner[None, :]) & (order[None, :] < order[:, None])
    return jnp.sum(jnp.where(earlier, counts[None, :], 0), axis=1)


def slot_prompts(owner, counts, slot_device, slot_index):
    order = jnp.arange(owner.shape[0], dtype=jnp.int32)
    first = first_slots(owner, counts)
    match = (
        (owner[None, :] == slot_device[:, None])
        & (first[None, :] <= slot_index[:, None])
        & (slot_index[:, None] < first[None, :] + counts[None, :])
    )
    present = jnp.any(match, axis=1)
    chosen = jnp.sum(jnp.where(match, order[None, :], 0), axis=1)
    return (chosen, present)


def softmax_state(scores, valid):
    scores = jnp.where(valid[:, None, None, :], scores, -1e30)
    peak = jnp.max(scores, axis=-1)
    weights = jnp.where(valid[:, None, None, :], jnp.exp(scores - peak[..., None]), 0.0)
    return (peak, jnp.sum(weights, axis=-1), weights.astype(jnp.bfloat16))


def state_each(query, keys, values, valid, scale):
    scores = jnp.einsum("sngd,slnd->sngl", query, keys, preferred_element_type=jnp.float32) * scale
    peak, total, rounded = softmax_state(scores, valid)
    mixed = jnp.einsum("sngl,slnd->sngd", rounded, values, preferred_element_type=jnp.float32)
    return (peak, total, mixed)


def state_shared(query, keys, values, valid, scale):
    scores = jnp.einsum("sngd,lnd->sngl", query, keys, preferred_element_type=jnp.float32) * scale
    peak, total, rounded = softmax_state(scores, valid)
    mixed = jnp.einsum("sngl,lnd->sngd", rounded, values, preferred_element_type=jnp.float32)
    return (peak, total, mixed)


def combine(first, second):
    peak = jnp.maximum(first[0], second[0])
    left_scale = jnp.exp(first[0] - peak)
    right_scale = jnp.exp(second[0] - peak)
    total = first[1] * left_scale + second[1] * right_scale
    mixed = first[2] * left_scale[..., None] + second[2] * right_scale[..., None]
    return (peak, total, mixed)


def on_device(
    prompt_hidden,
    norm_gain,
    kv_weight,
    prompt_excess,
    prompt_owner,
    response_counts,
    queries,
    new_kv,
    response_cache,
    positions,
    out_weight,
):
    device = lax.axis_index("dev")
    rows = prompt_hidden.shape[0]
    width = prompt_hidden.shape[1]
    local_heads = kv_weight.shape[1]
    head_size = kv_weight.shape[3]
    slots = queries.shape[0]
    query_heads = queries.shape[1]
    group = query_heads // local_heads
    prompt_count = prompt_excess.shape[0]
    scale = head_size ** (-0.5)
    token_index = device * rows + jnp.arange(rows, dtype=jnp.int32)
    member, offsets, starts, lengths = prompt_layout(prompt_excess, token_index)
    hidden = prompt_hidden.astype(jnp.float32)
    normed = (
        hidden * lax.rsqrt(jnp.mean(hidden * hidden, axis=-1, keepdims=True) + 1e-05) * norm_gain
    ).astype(jnp.bfloat16)
    projected = jnp.dot(
        normed,
        kv_weight.reshape(width, local_heads * 2 * head_size),
        preferred_element_type=jnp.float32,
    )
    projected = projected.reshape(rows, local_heads, 2, head_size)
    prompt_keys = rotate(projected[:, :, 0], offsets).astype(jnp.bfloat16)
    prompt_values = projected[:, :, 1].astype(jnp.bfloat16)
    grouped = queries.reshape(slots, local_heads, group, head_size)
    slot_index = jnp.arange(slots, dtype=jnp.int32)
    chosen, present = slot_prompts(
        prompt_owner, response_counts, jnp.zeros((slots,), jnp.int32) + device, slot_index
    )
    cache_valid = jnp.arange(response_cache.shape[1], dtype=jnp.int32)[None, :] < positions[:, None]
    cache_state = state_each(
        grouped, response_cache[:, :, :, 0], response_cache[:, :, :, 1], cache_valid, scale
    )
    self_valid = jnp.ones((slots, 1), dtype=bool)
    self_state = state_each(
        grouped, new_kv[:, None, :, 0], new_kv[:, None, :, 1], self_valid, scale
    )
    first = first_slots(prompt_owner, response_counts)
    rank = jnp.clip(slot_index - first[chosen], 0, RESP - 1)
    entry = chosen * RESP + rank
    select = (
        (entry[None, :] == jnp.arange(prompt_count * RESP, dtype=jnp.int32)[:, None])
        & present[None, :]
    ).astype(jnp.float32)
    table = jnp.dot(
        select,
        queries.reshape(slots, query_heads * head_size).astype(jnp.float32),
        precision=lax.Precision.HIGHEST,
    )
    table = lax.psum(table, "dev").astype(jnp.bfloat16)
    table = table.reshape(prompt_count, RESP, local_heads, group, head_size)
    held = jnp.any(member, axis=0)
    first_prompt = jnp.sum((starts + lengths <= token_index[0]).astype(jnp.int32))
    reach = min(rows // PROMPT_MIN + 2, prompt_count)
    layout = (
        jnp.full((prompt_count, RESP, local_heads, group), -1e30, jnp.float32),
        jnp.zeros((prompt_count, RESP, local_heads, group), jnp.float32),
        jnp.zeros((prompt_count, RESP, local_heads, group, head_size), jnp.float32),
    )
    for step in range(reach):
        pick = jnp.minimum(first_prompt + step, prompt_count - 1)
        live = (first_prompt + step < prompt_count) & held[pick]
        reply_queries = lax.dynamic_index_in_dim(table, pick, 0, keepdims=False)
        reply_live = jnp.arange(RESP, dtype=jnp.int32) < response_counts[pick]
        row_member = (token_index >= starts[pick]) & (token_index < starts[pick] + lengths[pick])
        valid = live & reply_live[:, None] & row_member[None, :]
        fresh = state_shared(reply_queries, prompt_keys, prompt_values, valid, scale)
        earlier = tuple(
            (lax.dynamic_index_in_dim(part_now, pick, 0, keepdims=False) for part_now in layout)
        )
        merged = combine(earlier, fresh)
        layout = tuple(
            (
                lax.dynamic_update_index_in_dim(part_now, part_new, pick, 0)
                for part_now, part_new in zip(layout, merged)
            )
        )
    joined_peak, joined_total, joined_mixed = merged_2(layout, "dev", combine)
    flat_peak = joined_peak.reshape(prompt_count * RESP, local_heads, group)
    flat_total = joined_total.reshape(prompt_count * RESP, local_heads, group)
    flat_mixed = joined_mixed.reshape(prompt_count * RESP, local_heads, group, head_size)
    own_peak = jnp.take(flat_peak, entry, axis=0)
    own_total = jnp.take(flat_total, entry, axis=0)
    own_mixed = jnp.take(flat_mixed, entry, axis=0)
    prompt_state = (
        jnp.where(present[:, None, None], own_peak, -1e30),
        jnp.where(present[:, None, None], own_total, 0.0),
        jnp.where(present[:, None, None, None], own_mixed, 0.0),
    )
    final = combine(combine(prompt_state, cache_state), self_state)
    attended = (
        (final[2] / final[1][..., None]).reshape(slots, query_heads, head_size).astype(jnp.bfloat16)
    )
    flat = attended.reshape(slots, query_heads * head_size)
    weight_flat = out_weight.reshape(query_heads * head_size, out_weight.shape[2])
    head_terms = jnp.dot(
        lax.all_gather(flat, "dev", axis=0, tiled=True),
        weight_flat,
        preferred_element_type=jnp.float32,
    )
    block_out = lax.psum_scatter(head_terms, "role", scatter_dimension=0, tiled=True).astype(
        jnp.bfloat16
    )
    return (attended, block_out)


def solution(mesh):
    return jax.shard_map(
        on_device,
        mesh=mesh,
        in_specs=(
            P(("groups", "dev"), None),
            P(),
            P(None, "role", None, None),
            P("groups"),
            P("groups"),
            P("groups"),
            P(("groups", "dev"), "role", None),
            P(("groups", "dev"), "role", None, None),
            P(("groups", "dev"), None, "role", None, None),
            P(("groups", "dev")),
            P("role", None, "dev"),
        ),
        out_specs=(P(("groups", "dev"), "role", None), P(("groups", "role"), "dev")),
        check_vma=False,
    )
```

profile of v0, /device:TPU:0, one launch (start us, length us, event | category | flops | bytes accessed | tf_op | source)
XLA Modules:
  0.0 298.8 jit_solution(10407446676272909244)
XLA Ops:
  7.2 0.5 slice.31
  7.8 0.7 broadcast_add_fusion
  8.4 0.2 reduce-window.8
  8.6 1.9 bitcast_subtract_fusion.3
  11.8 0.7 broadcast_compare_fusion
  12.5 0.9 select_reduce_fusion.2
  13.4 1.3 fusion.107
  14.8 0.6 fusion.110
  16.3 0.7 fusion.109
  17.0 0.6 fusion.108
  17.6 0.7 add.228
  18.4 0.7 gather_fusion
  19.0 0.9 fusion.46
  19.9 79.5 %psum.7 = bf16[20,1024]{1,0:T(8,128)(2,1)S(1)} all-reduce(f32[20,1024]{1,0:T(8,128)S(1)} %fusion.46), channel_id=1, replica_groups=mesh['groups'=1,'role'=2,'dev'=16] {'dev'}, use_global_device_ids=true, to_apply=%region_9.10 | all-reduce | flops 20480 | bytes 122880 | tf_op jit(solution)/shard_map/psum | solution.py:158
  99.5 7.2 %reshape.412 = bf16[4096,512]{1,0:T(8,128)(2,1)} reshape(bf16[4096,2,2,128]{3,2,1,0:T(2,128)(2,1)} %param.17) | data formatting | bytes 8388608 | tf_op jit(solution)/shard_map/reshape | solution.py:127
  106.7 6.6 %copy.138 = bf16[512,4096]{1,0:T(8,128)(2,1)} copy(bf16[512,4096]{0,1:T(8,128)(2,1)} %bitcast.222) | data formatting | bytes 8388608 | tf_op jit(solution)/shard_map/dot_general | solution.py:125
  113.3 0.5 fusion.3
  113.8 3.6 %fusion.7 = f32[256,2,2,128]{0,3,2,1:T(8,128)S(1)} fusion(bf16[2,2,128,4096]{3,2,1,0:T(8,128)(2,1)} %bitcast.223, bf16[256,4096]{1,0:T(8,128)(2,1)S(1)} %copy-done.1, f32[4096]{0:T(1024)S(1)} %copy-done.7, f32[256]{0:T(256)S(1)} %add_rsqrt_fusion), kind=kOutput, calls=%fused_computation.18 | convolution fusion | flops 1077936128 | bytes 6833152 | tf_op jit(solution)/shard_map/dot_general | solution.py:125
  119.9 1.2 compare_and_fusion
  121.2 0.3 multiply_cosine_fusion
  122.0 0.6 compare_and_fusion.3
  122.8 0.2 fusion.112
  123.0 0.2 fusion.39
  123.2 0.2 fusion.30
  124.1 0.6 compare_and_fusion.1
  124.7 0.2 fusion.113
  125.0 0.2 fusion.27
  125.3 0.6 copy-done.2
  126.0 10.2 %fusion.106 = (bf16[16,256,2,1,128]{4,3,2,1,0:T(2,128)(2,1)}, bf16[16,256,2,1,128]{4,3,2,1,0:T(2,128)(2,1)}) fusion(bf16[16,256,2,2,128]{4,3,2,1,0:T(2,128)(2,1)} %param.23), kind=kLoop, calls=%fused_computation.189 | loop fusion | bytes 8388608 | tf_op jit(solution)/shard_map/slice | solution.py:140
  136.3 2.9 fusion.111
  139.4 0.1 fusion.59
  139.6 0.2 fusion.32
  139.9 0.2 fusion.41
  140.1 37.8 %all_gather.32 = f32[16,4,5,2,4]{2,4,3,1,0:T(4,128)S(1)} all-gather(f32[1,4,5,2,4]{2,4,3,1,0:T(4,128)S(1)} %get-tuple-element.219), channel_id=1, replica_groups=mesh['groups'=1,'role'=2,'dev'=16] {'dev'}, dimensions={0}, use_global_device_ids=true | all-gather | bytes 10880 | tf_op jit(solution)/shard_map/all_gather | solution.py:14
  177.9 38.5 %all_gather.29 = f32[16,4,5,2,4]{2,4,3,1,0:T(4,128)S(1)} all-gather(f32[1,4,5,2,4]{2,4,3,1,0:T(4,128)S(1)} %get-tuple-element.220), channel_id=1, replica_groups=mesh['groups'=1,'role'=2,'dev'=16] {'dev'}, dimensions={0}, use_global_device_ids=true | all-gather | bytes 10880 | tf_op jit(solution)/shard_map/all_gather | solution.py:14
  216.5 0.9 slice_bitcast_fusion.1
  217.4 22.4 %while.19 = (s32[]{:T(128)}, f32[4,5,2,4]{1,3,2,0:T(4,128)S(1)}, f32[4,5,2,4]{1,3,2,0:T(4,128)S(1)}, f32[4,5,2,4,128]{4,3,2,1,0:T(4,128)S(1)}, f32[16,4,5,2,4]{2...) while((s32[]{:T(128)}, f32[4,5,2,4]{1,3,2,0:T(4,128)S(1)}, ...), condition=%wide.region_15.16_spmd, body=%wide.region_14.15_spmd.sunk | while | flops 62405 | bytes 254871 | solution.py:19
  217.4 0.1 copy.236
  217.7 1.2 fusion.123
  219.2 1.2 fusion.123
  220.7 1.2 fusion.123
  221.9 0.1 copy.236
  222.2 1.2 fusion.123
  223.7 1.2 fusion.123
  225.2 1.2 fusion.123
  226.7 1.2 fusion.123
  228.2 1.2 fusion.123
  229.7 1.2 fusion.123
  231.2 1.2 fusion.123
  232.7 1.2 fusion.123
  234.2 1.2 fusion.123
  235.4 0.1 copy.236
  235.7 1.2 fusion.123
  236.9 0.1 copy.236
  237.2 1.2 fusion.123
  238.7 1.2 fusion.123
  240.0 0.6 gather_fusion.2
  240.8 0.6 gather_fusion.3
  242.1 0.6 gather_fusion.1
  242.7 2.7 fusion.24
  245.4 38.6 %all_gather.36 = bf16[256,1024]{1,0:T(8,128)(2,1)S(1)} all-gather(bf16[16,1024]{1,0:T(8,128)(2,1)S(1)} %convert_element_type.68), channel_id=1, replica_groups=mesh['groups'=1,'role'=2,'dev'=16] {'dev'}, dimensions={0}, use_global_device_ids=true | all-gather | bytes 557056 | tf_op jit(solution)/shard_map/all_gather | solution.py:205
  284.0 1.0 fusion.114
  285.1 5.3 %reduce-scatter.2.cloned.1.call-done = f32[128,256]{1,0:T(8,128)} async-done(((f32[256,256]{1,0:T(8,128)}), f32[128,256]{1,0:T(8,128)}) %reduce-scatter.2.cloned.1.call-update) | async-done | bytes 131088 | tf_op jit(solution)/shard_map/reduce_scatter | solution.py:209
  290.4 1.5 convert_element_type.69
  (116 shorter events, 6.6 us)
Async XLA Ops:
  7.2 276.9 %copy-start = (bf16[8,128,256]{2,1,0:T(8,128)(2,1)S(1)}, bf16[8,128,256]{2,1,0:T(8,128)(2,1)}, u32[]{:S(2)}) copy-start(bf16[8,128,256]{2,1,0:T(8,128)(2,1)} %param.25) | copy-start | bytes 1572868
  7.2 209.3 %all-gather.2.cloned.1.call-start = ((), (), s32[]{:S(2)}) async-start(), calls=%async_computation.1 | async-start | bytes 1392640 | tf_op jit(solution)/shard_map/all_gather | solution.py:14
  106.7 6.6 %copy-start.1 = (bf16[256,4096]{1,0:T(8,128)(2,1)S(1)}, bf16[256,4096]{1,0:T(8,128)(2,1)}, u32[]{:S(2)}) copy-start(bf16[256,4096]{1,0:T(8,128)(2,1)} %param.15) | copy-start | bytes 6291460
  106.7 7.1 %copy-start.7 = (f32[4096]{0:T(1024)S(1)}, f32[4096]{0:T(1024)}, u32[]{:S(2)}) copy-start(f32[4096]{0:T(1024)} %param.16) | copy-start | bytes 49156
  125.3 0.6 copy-start.2
  125.9 10.3 %copy-start.6 = (s32[16]{0:T(128)S(1)}, s32[16]{0:T(128)}, u32[]{:S(2)}) copy-start(s32[16]{0:T(128)} %param.24) | copy-start | bytes 196
  125.9 10.3 %copy-start.5 = (bf16[16,8,128]{2,1,0:T(8,128)(2,1)S(1)}, bf16[16,8,128]{2,1,0:T(8,128)(2,1)}, u32[]{:S(2)}) copy-start(bf16[16,8,128]{2,1,0:T(8,128)(2,1)} %param.21) | copy-start | bytes 98308
  126.0 13.4 %copy-start.3 = (bf16[16,2,2,128]{3,2,1,0:T(2,128)(2,1)S(1)}, bf16[16,2,2,128]{3,2,1,0:T(2,128)(2,1)}, u32[]{:S(2)}) copy-start(bf16[16,2,2,128]{3,2,1,0:T(2,128)(2,1)} %param.22) | copy-start | bytes 49156
  126.0 164.4 %reduce-scatter.2.cloned.1.call-start = ((), (), s32[]{:S(2)}) async-start(), calls=%async_computation.2 | async-start | bytes 393216 | tf_op jit(solution)/shard_map/reduce_scatter | solution.py:209
  245.4 46.5 %copy-start.4 = (bf16[16,2,4,128]{3,2,1,0:T(4,128)(2,1)}, bf16[16,2,4,128]{3,2,1,0:T(4,128)(2,1)S(1)}, u32[]{:S(2)}) copy-start(bf16[16,2,4,128]{3,2,1,0:T(4,128)(2,1)S(1)} %fusion.24) | copy-start | bytes 98308
Sparse Core Ops, SparseCore 0:
  126.1 53.9 all-gather.1
  285.2 5.1 reduce-scatter.1
where the time goes:
time: 300 us; the launch traced here: 299 us
  blocking collectives  194 us (65%)
  local copies, waits for them, and re-layouts  37.2 us (12%)
  other arithmetic  29.3 us (10%)
  between operations  20.1 us (7%)
  matrix products  12 us (4%)
  waiting for transfers between devices  5.37 us (2%)
    psum x1, blocking collectives, on_device(): table = lax.psum(table, 'dev').astype(jnp.bfloat16)  79.5 us
    all_gather x2, blocking collectives, merged_2(): gathered = jax.tree.map(lambda a: lax.all_gather(a, axis), part)  76.3 us
    all_gather x1, blocking collectives, on_device(): lax.all_gather(flat, 'dev', axis=0, tiled=True)  38.6 us
    add x15, other arithmetic, combine(): first[2] * left_scale[..., None] + second[2] * right_scale[..., None]  17.5 us
    slice x1, local copies, waits for them, and re-layouts, on_device(): response_cache[:, :, :, 0]  10.2 us
    reshape x1, local copies, waits for them, and re-layouts, on_device(): kv_weight.reshape(width, local_heads * 2 * head_size)  7.22 us
    dot_general x1, local copies, waits for them, and re-layouts, on_device(): jnp.dot(normed, kv_weight.reshape(width, local_heads * 2 * head_size), pr...  6.6 us
  transfers between devices with their start and end apart: 2, of which 1 were waited for; matrix products, arithmetic and copies ran while one was open for 5% of the time, Pallas kernels for 0%

commit v1 on v0

v1 whole, which is shorter than its diff:
```python
import functools

import jax
import jax.numpy as jnp
import numpy as np
from jax import lax
from jax.experimental import pallas as pl
from jax.experimental.pallas import tpu as pltpu
from jax.sharding import PartitionSpec as P

RESP = 5
PROMPT_MIN = 512
ROPE_BASE = 500000.0
EPS = 1e-05
LOW = -1e30
LANES = 128

SMEM = pl.BlockSpec(memory_space=pltpu.SMEM)
VMEM = pl.BlockSpec(memory_space=pltpu.VMEM)
ANY = pl.BlockSpec(memory_space=pl.ANY)
NT = (((1,), (1,)), ((), ()))
NN = (((1,), (0,)), ((), ()))


def cost(flops, bytes_accessed):
    return pl.CostEstimate(flops=flops, bytes_accessed=bytes_accessed, transcendentals=0)


def params(mib=48):
    return pltpu.CompilerParams(vmem_limit_bytes=mib << 20)


def phases(n):
    found, stride = [], 1
    while n > 1:
        radix = 4 if n % 4 == 0 else 2
        assert n % radix == 0
        found.append((stride, radix))
        stride, n = stride * radix, n // radix
    return found


def exchange(x, phase):
    stride, radix = phase
    n = lax.axis_size("dev")
    return [
        lax.ppermute(x, "dev", [(i, i ^ (k * stride)) for i in range(n)]) for k in range(1, radix)
    ]


def dot(a, b, dims):
    return lax.dot_general(a, b, dims, preferred_element_type=jnp.float32)


def first_slot(owner, counts, p):
    total = jnp.int32(0)
    for q in range(p):
        total = total + jnp.where(owner[q] == owner[p], counts[q], 0)
    return total


def digit(index, phase):
    stride, radix = phase
    return lax.rem(lax.div(index, stride), radix)


def cache_kernel(per, pos_ref, q_ref, new_ref, cache_ref, out_ref, o_ref, lse_ref, att):
    slots, heads, size = q_ref.shape
    ways = new_ref.shape[1]
    group = heads // (ways // 2)
    rows = cache_ref.shape[1]
    scale = size ** (-0.5)
    step = pl.program_id(0)
    head = lax.broadcasted_iota(jnp.int32, (heads, 1), 0) // group
    column = lax.broadcasted_iota(jnp.int32, (heads, rows), 1)
    mine = (column % ways) == 2 * head
    for i in range(per):
        s = step * per + i
        q = q_ref[s]
        scores = dot(q, cache_ref[i], NT) * scale
        valid = mine & (column < pos_ref[s] * ways)
        scores = jnp.where(valid, scores, LOW)
        fresh = new_ref[s].astype(jnp.float32)
        key = jnp.zeros((heads, size), jnp.float32)
        value = jnp.zeros((heads, size), jnp.float32)
        for n in range(ways // 2):
            key = jnp.where(head == n, fresh[2 * n : 2 * n + 1, :], key)
            value = jnp.where(head == n, fresh[2 * n + 1 : 2 * n + 2, :], value)
        own = jnp.sum(q.astype(jnp.float32) * key, axis=1, keepdims=True) * scale
        peak = jnp.maximum(jnp.max(scores, axis=1, keepdims=True), own)
        weights = jnp.where(valid, jnp.exp(scores - peak), 0.0)
        alone = jnp.exp(own - peak)
        total = jnp.sum(weights, axis=1, keepdims=True) + alone
        moved = pltpu.roll(weights, 1, axis=1).astype(jnp.bfloat16)
        mixed = dot(moved, cache_ref[i], NN)
        mixed = mixed + alone.astype(jnp.bfloat16).astype(jnp.float32) * value
        mixed = mixed / total
        o_ref[s] = mixed
        lse_ref[s] = jnp.broadcast_to(peak + jnp.log(total), (heads, size))
        att[pl.ds(s, heads, stride=slots), :] = mixed

    @pl.when(step == pl.num_programs(0) - 1)
    def _():
        out_ref[...] = att[...].astype(out_ref.dtype)


def cache_attention(positions, queries, new_kv, response_cache):
    slots, heads, size = queries.shape
    ctx, kv = response_cache.shape[1], response_cache.shape[2]
    rows = ctx * kv * 2
    per = 2
    whole = lambda *shape: pl.BlockSpec(shape, lambda i: (0,) * len(shape))
    f32 = jnp.float32
    return pl.pallas_call(
        functools.partial(cache_kernel, per),
        grid=(slots // per,),
        in_specs=[
            SMEM,
            whole(slots, heads, size),
            whole(slots, kv * 2, size),
            pl.BlockSpec((per, rows, size), lambda i: (i, 0, 0)),
        ],
        out_specs=[
            whole(slots * heads, size),
            whole(slots, heads, size),
            whole(slots, heads, size),
        ],
        out_shape=[
            jax.ShapeDtypeStruct((slots * heads, size), jnp.bfloat16),
            jax.ShapeDtypeStruct((slots, heads, size), f32),
            jax.ShapeDtypeStruct((slots, heads, size), f32),
        ],
        scratch_shapes=[pltpu.VMEM((slots * heads, size), f32)],
        compiler_params=params(),
        cost_estimate=cost(10_000_000_000, slots * rows * size * 2),
        name="cache_attention",
    )(
        positions,
        queries,
        new_kv.reshape(slots, kv * 2, size),
        response_cache.reshape(slots, rows, size),
    )


def project_kernel(
    chunks, excess, hid_hbm, gain_ref, freq_ref, w_hbm, k_ref, v_ref, hid, w, wide, acc, hsem, wsem
):
    rows, width = hid.shape
    size = w.shape[1]
    ways = w.shape[0] // width
    depth = width // chunks
    load = pltpu.make_async_copy(hid_hbm, hid, hsem)
    load.start()
    loads = []
    for c in range(chunks):
        part = pl.ds(c * depth * ways, depth * ways)
        loads.append(pltpu.make_async_copy(w_hbm.at[part, :], w.at[part, :], wsem.at[c]))
        loads[-1].start()
    token = lax.axis_index("dev") * rows + lax.broadcasted_iota(jnp.int32, (rows, size), 0)
    offset, start = token, jnp.int32(0)
    for p in range(excess.shape[0]):
        offset = jnp.where(token >= start, token - start, offset)
        start = start + PROMPT_MIN + excess[p]
    angle = offset.astype(jnp.float32) * freq_ref[...]
    lane = lax.broadcasted_iota(jnp.int32, (rows, size), 1)
    cosine = jnp.cos(angle)
    sine = jnp.where(lane < size // 2, -1.0, 1.0) * jnp.sin(angle)
    load.wait()
    total = jnp.zeros((rows, 1), jnp.float32)
    for c in range(chunks):
        x = hid[:, c * depth : (c + 1) * depth].astype(jnp.float32)
        total = total + jnp.sum(x * x, axis=1, keepdims=True)
    inverse = lax.rsqrt(total / width + EPS)
    for c in range(chunks):
        at = slice(c * depth, (c + 1) * depth)
        x = hid[:, at].astype(jnp.float32) * inverse * gain_ref[:, at]
        x = x.astype(jnp.bfloat16)
        loads[c].wait()
        buffer = wide.at[c % 2]
        buffer[...] = w[c * depth * ways : (c + 1) * depth * ways, :].astype(jnp.float32)
        parts = [
            buffer[pl.ds(j, depth, stride=ways), :].astype(jnp.bfloat16) for j in range(ways)
        ]
        term = dot(x, jnp.concatenate(parts, axis=1), NN)
        if c == 0:
            acc[...] = term
        else:
            acc[...] += term
    for n in range(ways // 2):
        key = acc[:, 2 * n * size : (2 * n + 1) * size]
        turned = key * cosine + pltpu.roll(key, size // 2, axis=1) * sine
        k_ref[n] = turned.astype(k_ref.dtype)
        v_ref[n] = acc[:, (2 * n + 1) * size : (2 * n + 2) * size].astype(v_ref.dtype)


def project(prompt_hidden, norm_gain, kv_weight, prompt_excess):
    rows, width = prompt_hidden.shape
    kv, size = kv_weight.shape[1], kv_weight.shape[3]
    ways = kv * 2
    chunks = 8
    depth = width // chunks
    half = np.arange(size // 2, dtype=np.float64)
    freq = ROPE_BASE ** (-2.0 * half / size)
    freq = jnp.asarray(np.concatenate([freq, freq])[None, :], jnp.float32)
    f32, bf16 = jnp.float32, jnp.bfloat16
    return pl.pallas_call(
        functools.partial(project_kernel, chunks),
        in_specs=[SMEM, ANY, VMEM, VMEM, ANY],
        out_specs=[VMEM, VMEM],
        out_shape=[jax.ShapeDtypeStruct((kv, rows, size), bf16)] * 2,
        scratch_shapes=[
            pltpu.VMEM((rows, width), bf16),
            pltpu.VMEM((width * ways, size), bf16),
            pltpu.VMEM((2, depth * ways, size), f32),
            pltpu.VMEM((rows, ways * size), f32),
            pltpu.SemaphoreType.DMA,
            pltpu.SemaphoreType.DMA((chunks,)),
        ],
        compiler_params=params(),
        cost_estimate=cost(10_000_000_000, width * (rows + ways * size) * 2),
        name="project",
    )(
        prompt_excess,
        prompt_hidden,
        norm_gain[None, :],
        freq,
        kv_weight.reshape(width * ways, size),
    )


def pick_tile(refs, owner, phase, index):
    own = digit(lax.axis_index("dev"), phase)
    tile = refs[0][index]
    for k in range(1, len(refs)):
        tile = jnp.where(digit(owner, phase) == jnp.bitwise_xor(own, k), refs[k][index], tile)
    return tile


def slot_of(owner, counts, p, r, slots):
    return jnp.minimum(first_slot(owner, counts, p) + r, slots - 1)


def table_kernel(phase, raw, carried, owner, counts, *refs):
    radix = phase[1]
    sources, out = refs[:radix], refs[-1]
    entries = owner.shape[0] * RESP
    slots = sources[0].shape[0]
    for p in range(owner.shape[0]):
        for r in range(RESP):
            index = slot_of(owner, counts, p, r, slots) if raw else p * RESP + r
            out[p * RESP + r] = pick_tile(sources, owner[p], phase, index)
    at = entries
    if raw:
        local = refs[radix]
        out[at : at + local.shape[0]] = local[...]
    else:
        for source in sources:
            out[at : at + carried] = source[entries : entries + carried]
            at += carried


def make_table(phase, raw, carried, owner, counts, sources, local):
    heads, size = sources[0].shape[1:]
    entries = owner.shape[0] * RESP
    extra = local.shape[0] if raw else carried * len(sources)
    args = list(sources) + ([local] if raw else [])
    return pl.pallas_call(
        functools.partial(table_kernel, phase, raw, carried),
        in_specs=[SMEM, SMEM] + [VMEM] * len(args),
        out_specs=VMEM,
        out_shape=jax.ShapeDtypeStruct((entries + extra, heads, size), sources[0].dtype),
        compiler_params=params(),
        cost_estimate=cost(100_000_000, 200_000),
        name="make_table",
    )(owner, counts, *args)


def stat_rows(rows):
    return 16 * pl.cdiv(3 * pl.cdiv(rows, LANES), 16)


def put_state(out, mixed, lse, rows):
    out[:rows, :] = mixed.astype(out.dtype)
    count = pl.cdiv(rows, LANES)
    line = lax.broadcasted_iota(jnp.int32, (LANES, LANES), 0)
    lane = lax.broadcasted_iota(jnp.int32, (LANES, LANES), 1)
    place = lax.broadcasted_iota(jnp.int32, (stat_rows(rows), LANES), 0)
    stats = jnp.zeros((stat_rows(rows), LANES), jnp.float32)
    for b in range(count):
        size = min(LANES, rows - b * LANES)
        eye = line[:size] == lane[:size]
        rest = jnp.sum(
            jnp.where(eye, lse[b * LANES : b * LANES + size, :], 0.0), axis=0, keepdims=True
        )
        for k in range(3):
            term = rest.astype(jnp.bfloat16).astype(jnp.float32)
            stats = jnp.where(place == 3 * b + k, term, stats)
            rest = rest - term
    out[rows : rows + stat_rows(rows), :] = stats.astype(out.dtype)


def get_lse(message, rows):
    stats = message[rows : rows + stat_rows(rows), :].astype(jnp.float32)
    line = lax.broadcasted_iota(jnp.int32, (LANES, LANES), 0)
    lane = lax.broadcasted_iota(jnp.int32, (LANES, LANES), 1)
    blocks = []
    for b in range(pl.cdiv(rows, LANES)):
        size = min(LANES, rows - b * LANES)
        row = (stats[3 * b : 3 * b + 1] + stats[3 * b + 1 : 3 * b + 2]) + stats[3 * b + 2 : 3 * b + 3]
        eye = line[:size] == lane[:size]
        blocks.append(jnp.sum(jnp.where(eye, row, 0.0), axis=1, keepdims=True))
    return jnp.concatenate(blocks, axis=0) if len(blocks) > 1 else blocks[0]


def merge(messages, rows):
    lses = [get_lse(m, rows) for m in messages]
    peak = functools.reduce(jnp.maximum, lses)
    total = jnp.zeros_like(peak)
    mixed = None
    for m, lse in zip(messages, lses):
        weight = jnp.exp(lse - peak)
        total = total + weight
        term = m[:rows, :].astype(jnp.float32) * weight
        mixed = term if mixed is None else mixed + term
    return mixed / total, peak + jnp.log(total)


def prompt_kernel(
    phase, raw, carried, excess, owner, counts, k_ref, v_ref, o_ref, lse_ref, *refs
):
    radix = phase[1]
    sources, out, table, mine_o, mine_lse = refs[:radix], refs[-4], refs[-3], refs[-2], refs[-1]
    kv, tokens, size = k_ref.shape
    slots, heads, _ = o_ref.shape
    group = heads // kv
    prompts = owner.shape[0]
    rows = prompts * RESP * heads
    me = lax.axis_index("dev")
    for p in range(prompts):
        here = owner[p] == me
        for r in range(RESP):
            t = p * RESP + r
            slot = slot_of(owner, counts, p, r, slots)
            tile = pick_tile(sources, owner[p], phase, slot if raw else t)
            table[t * heads : (t + 1) * heads, :] = tile.astype(jnp.float32)
            mine_o[t * heads : (t + 1) * heads, :] = o_ref[slot]
            mine_lse[t * heads : (t + 1) * heads, :] = jnp.where(here, lse_ref[slot], LOW)
    queries = table[...].astype(jnp.bfloat16)
    head = (lax.broadcasted_iota(jnp.int32, (rows, 1), 0) % heads) // group
    scores = dot(queries, k_ref[0], NT)
    for n in range(1, kv):
        scores = jnp.where(head == n, dot(queries, k_ref[n], NT), scores)
    token = me * tokens + lax.broadcasted_iota(jnp.int32, (1, tokens), 1)
    start = jnp.int32(0)
    valid = []
    for p in range(prompts):
        end = start + PROMPT_MIN + excess[p]
        inside = ((token >= start) & (token < end)).astype(jnp.float32)
        valid.append(jnp.broadcast_to(inside, (RESP * heads, tokens)))
        start = end
    valid = jnp.concatenate(valid, axis=0) > 0.5
    scores = jnp.where(valid, scores * size ** (-0.5), LOW)
    peak = jnp.max(scores, axis=1, keepdims=True)
    weights = jnp.where(valid, jnp.exp(scores - peak), 0.0)
    total = jnp.sum(weights, axis=1, keepdims=True)
    weights = weights.astype(jnp.bfloat16)
    mixed = dot(weights, v_ref[0], NN)
    for n in range(1, kv):
        mixed = jnp.where(head == n, dot(weights, v_ref[n], NN), mixed)
    other = mine_lse[...]
    top = jnp.maximum(other, peak)
    left = jnp.exp(peak - top)
    right = jnp.exp(other - top)
    total = total * left + right
    mixed = (mixed * left + mine_o[...] * right) / total
    put_state(out, mixed, top + jnp.log(total), rows)
    at = rows + stat_rows(rows)
    entries = prompts * RESP
    for source in sources:
        block = source[entries : entries + carried] if not raw else source[...]
        out[at : at + carried * heads, :] = block.reshape(carried * heads, size)
        at += carried * heads


def prompt_attention(phase, carried, excess, owner, counts, keys, values, o, lse, sources):
    heads, size = o.shape[1:]
    rows = owner.shape[0] * RESP * heads
    total = rows + stat_rows(rows) + carried * heads * len(sources)
    f32 = jnp.float32
    return pl.pallas_call(
        functools.partial(prompt_kernel, phase, False, carried),
        in_specs=[SMEM] * 3 + [VMEM] * (4 + len(sources)),
        out_specs=VMEM,
        out_shape=jax.ShapeDtypeStruct((total, size), jnp.bfloat16),
        scratch_shapes=[pltpu.VMEM((rows, size), f32)] * 3,
        compiler_params=params(),
        cost_estimate=cost(2_000_000_000, 500_000),
        name="prompt_attention",
    )(excess, owner, counts, keys, values, o, lse, *sources)


def merge_kernel(rows, *refs):
    mixed, lse = merge(refs[:-1], rows)
    put_state(refs[-1], mixed, jnp.broadcast_to(lse, mixed.shape), rows)


def merge_states(rows, messages):
    size = messages[0].shape[1]
    return pl.pallas_call(
        functools.partial(merge_kernel, rows),
        in_specs=[VMEM] * len(messages),
        out_specs=VMEM,
        out_shape=jax.ShapeDtypeStruct((rows + stat_rows(rows), size), jnp.bfloat16),
        compiler_params=params(),
        cost_estimate=cost(1_000_000_000, 500_000),
        name="merge_states",
    )(*messages)


def base_kernel(offsets, skip, slots, w_ref, *refs):
    sources, keep, give, lhs = refs[:-3], refs[-3], refs[-2], refs[-1]
    heads, size, _ = w_ref.shape
    me = lax.axis_index("dev")
    block = slots * heads
    per = len(offsets) // len(sources)
    for i, offset in enumerate(offsets):
        at = pl.multiple_of(jnp.bitwise_xor(me, offset) * slots, slots)
        begin = skip + (i % per) * block
        for h in range(heads):
            lhs[pl.ds(at, slots), h * size : (h + 1) * size] = sources[i // per][
                begin + h * slots : begin + (h + 1) * slots, :
            ]
    half = keep.shape[0]
    role = lax.axis_index("role")
    weight = w_ref[...].reshape(heads * size, w_ref.shape[2])
    keep[...] = dot(lhs[pl.ds(pl.multiple_of(role * half, half), half), :], weight, NN)
    give[...] = dot(lhs[pl.ds(pl.multiple_of((1 - role) * half, half), half), :], weight, NN)


def base_product(offsets, skip, slots, weight, sources):
    heads, size, columns = weight.shape
    total = len(offsets) * slots
    half = jax.ShapeDtypeStruct((total // 2, columns), jnp.float32)
    return pl.pallas_call(
        functools.partial(base_kernel, offsets, skip, slots),
        in_specs=[VMEM] * (1 + len(sources)),
        out_specs=[VMEM, VMEM],
        out_shape=[half, half],
        scratch_shapes=[pltpu.VMEM((total, heads * size), jnp.bfloat16)],
        compiler_params=params(),
        cost_estimate=cost(2_000_000_000, 1_000_000),
        name="base_product",
    )(weight, *sources)


def answer_kernel(rows, owner, counts, w_ref, o_ref, *refs):
    messages, att_ref, part, joined = refs[:-3], refs[-3], refs[-2], refs[-1]
    heads, size, columns = w_ref.shape
    slots = o_ref.shape[0]
    entries = rows // heads
    mixed, _ = merge(messages, rows)
    joined[...] = mixed
    att_ref[...] = o_ref[...].astype(att_ref.dtype)
    me = lax.axis_index("dev")
    for p in range(owner.shape[0]):
        for r in range(RESP):
            t = p * RESP + r

            @pl.when((owner[p] == me) & (r < counts[p]))
            def _():
                tile = joined[t * heads : (t + 1) * heads, :]
                att_ref[slot_of(owner, counts, p, r, slots)] = tile.astype(att_ref.dtype)

    total = None
    for h in range(heads):
        lhs = joined[pl.ds(h, entries, stride=heads), :].astype(jnp.bfloat16)
        term = dot(lhs, w_ref[h], NN)
        total = term if total is None else total + term
    part[:entries, :] = total


def answer_product(rows, owner, counts, weight, o, messages):
    heads, size, columns = weight.shape
    entries = rows // heads
    return pl.pallas_call(
        functools.partial(answer_kernel, rows),
        in_specs=[SMEM, SMEM] + [VMEM] * (2 + len(messages)),
        out_specs=[VMEM, VMEM],
        out_shape=[
            jax.ShapeDtypeStruct(o.shape, jnp.bfloat16),
            jax.ShapeDtypeStruct((8 * pl.cdiv(entries, 8), columns), jnp.float32),
        ],
        scratch_shapes=[pltpu.VMEM((rows, size), jnp.float32)],
        compiler_params=params(),
        cost_estimate=cost(1_000_000_000, 1_000_000),
        name="answer_product",
    )(owner, counts, weight, o, *messages)


def finish_kernel(slots, owner, counts, keep, taken, part, part_taken, out, wide):
    half = keep.shape[0]
    begin = lax.axis_index("role") * half
    wide[...] = keep[...] + taken[...]
    for p in range(owner.shape[0]):
        for r in range(RESP):
            t = p * RESP + r
            row = owner[p] * slots + slot_of(owner, counts, p, r, slots) - begin

            @pl.when((r < counts[p]) & (row >= 0) & (row < half))
            def _():
                wide[pl.ds(row, 1), :] = part[t : t + 1, :] + part_taken[t : t + 1, :]

    out[...] = wide[...].astype(out.dtype)


def finish(slots, owner, counts, keep, taken, part, part_taken):
    return pl.pallas_call(
        functools.partial(finish_kernel, slots),
        in_specs=[SMEM, SMEM] + [VMEM] * 4,
        out_specs=VMEM,
        out_shape=jax.ShapeDtypeStruct(keep.shape, jnp.bfloat16),
        scratch_shapes=[pltpu.VMEM(keep.shape, jnp.float32)],
        compiler_params=params(),
        name="finish",
    )(owner, counts, keep, taken, part, part_taken)


def swap_role(x):
    return lax.ppermute(x, "role", [(0, 1), (1, 0)])


def on_device(
    prompt_hidden,
    norm_gain,
    kv_weight,
    excess,
    owner,
    counts,
    queries,
    new_kv,
    response_cache,
    positions,
    out_weight,
):
    slots, heads, size = queries.shape
    steps = phases(lax.axis_size("dev"))
    rows = owner.shape[0] * RESP * heads
    received = [queries] + exchange(queries, steps[0])
    local, o, lse = cache_attention(positions, queries, new_kv, response_cache)
    local = local.reshape(slots, heads, size)
    offsets = [0]
    carried = slots
    raw = True
    for before, phase in zip(steps[:-1], steps[1:]):
        message = make_table(before, raw, carried, owner, counts, received, local)
        received = [message] + exchange(message, phase)
        carried = carried if raw else carried * before[1]
        offsets = [k * phase[0] ^ a for k in range(phase[1]) for a in offsets]
        raw = False
    keys, values = project(prompt_hidden, norm_gain, kv_weight, excess)
    message = prompt_attention(
        steps[-1], carried, excess, owner, counts, keys, values, o, lse, received
    )
    received = [message] + exchange(message, steps[0])
    offsets = [k * steps[0][0] ^ a for k in range(steps[0][1]) for a in offsets]
    blocks = received
    for phase in steps[1:]:
        message = merge_states(rows, received)
        received = [message] + exchange(message, phase)
    keep, give = base_product(offsets, rows + stat_rows(rows), slots, out_weight, blocks)
    taken = swap_role(give)
    attended, part = answer_product(rows, owner, counts, out_weight, o, received)
    block_out = finish(slots, owner, counts, keep, taken, part, swap_role(part))
    return (attended, block_out)


def solution(mesh):
    return jax.shard_map(
        on_device,
        mesh=mesh,
        in_specs=(
            P(("groups", "dev"), None),
            P(),
            P(None, "role", None, None),
            P("groups"),
            P("groups"),
            P("groups"),
            P(("groups", "dev"), "role", None),
            P(("groups", "dev"), "role", None, None),
            P(("groups", "dev"), None, "role", None, None),
            P(("groups", "dev")),
            P("role", None, "dev"),
        ),
        out_specs=(P(("groups", "dev"), "role", None), P(("groups", "role"), "dev")),
        check_vma=False,
    )
```

time: 300 us -> 53.5 us (0.18)
  blocking collectives: 194 us -> 0 us
  local copies, waits for them, and re-layouts: 37.2 us -> 4.35 us
  other arithmetic: 29.3 us -> 0 us
  between operations: 20.1 us -> 0.83 us
  Pallas kernels: 0 us -> 17.6 us
  starting transfers between devices: 0.08 us -> 17.3 us
  matrix products: 12 us -> 0 us
  waiting for transfers between devices: 5.37 us -> 13.1 us
    all_gather x3 -> x0, blocking collectives: 115 us -> none  [the longest x2 76.3 us: merged_2(): gathered = jax.tree.map(lambda a: lax.all_gather(a, axis), part)]
    psum x1 -> x0, blocking collectives: 79.5 us -> none  [on_device(): table = lax.psum(table, 'dev').astype(jnp.bfloat16)]
    add x34 -> x0, other arithmetic: 19.4 us -> none  [the longest x15 17.5 us: combine(): first[2] * left_scale[..., None] + second[2] * right_scale[..., None]]
    pallas_call x0 -> x8, Pallas kernels: none -> 17.6 us  [the longest x1 7.42 us: cache_attention(): pl.pallas_call(functools.partial(cache_kernel, per), grid=(slots // per,)...]
    ppermute x0 -> x14, starting transfers between devices: none -> 17.3 us  [the longest x12 17.3 us: exchange(): lax.ppermute(x, 'dev', [(i, i ^ k * stride) for i in range(n)])]
    ppermute x0 -> x14, waiting for transfers between devices: none -> 13.1 us  [the longest x12 11.9 us: exchange(): lax.ppermute(x, 'dev', [(i, i ^ k * stride) for i in range(n)])]
    dot_general x10 -> x0, matrix products: 12 us -> none  [the longest x1 3.56 us: on_device(): jnp.dot(normed, kv_weight.reshape(width, local_heads * 2 * head_size), pr...]
    slice x2 -> x0, local copies, waits for them, and re-layouts: 10.7 us -> none  [the longest x1 10.2 us: on_device(): response_cache[:, :, :, 0]]
  transfers between devices with their start and end apart: 2 -> 14, of which waited for: 1 -> 7; matrix products, arithmetic and copies ran while one was open for 5% -> 0% of each run, Pallas kernels for 0% -> 27%
where the time goes in v1:
time: 53.5 us; the launch traced here: 53.2 us
  Pallas kernels  17.6 us (33%)
  starting transfers between devices  17.3 us (32%)
  waiting for transfers between devices  13.1 us (24%)
  local copies, waits for them, and re-layouts  4.35 us (8%)
  between operations  0.83 us (2%)
    ppermute x12, starting transfers between devices, exchange(): lax.ppermute(x, 'dev', [(i, i ^ k * stride) for i in range(n)])  17.3 us
    ppermute x12, waiting for transfers between devices, exchange(): lax.ppermute(x, 'dev', [(i, i ^ k * stride) for i in range(n)])  11.9 us
    pallas_call x1, Pallas kernels, cache_attention(): pl.pallas_call(functools.partial(cache_kernel, per), grid=(slots // per,)...  7.42 us
    pallas_call x1, Pallas kernels, project(): pl.pallas_call(functools.partial(project_kernel, chunks), in_specs=[SMEM,...  4.5 us
    unnamed x24, local copies, waits for them, and re-layouts  4.35 us
    pallas_call x1, Pallas kernels, answer_product(): pl.pallas_call(functools.partial(answer_kernel, rows), in_specs=[SMEM, SM...  1.8 us
    pallas_call x1, Pallas kernels, finish(): pl.pallas_call(functools.partial(finish_kernel, slots), in_specs=[SMEM, S...  1.47 us
    ppermute x2, waiting for transfers between devices, swap_role(): return lax.ppermute(x, 'role', [(0, 1), (1, 0)])  1.2 us
  transfers between devices with their start and end apart: 14, of which 7 were waited for; matrix products, arithmetic and copies ran while one was open for 0% of the time, Pallas kernels for 27%

profile of v1, /device:TPU:0, one launch (start us, length us, event | category | flops | bytes accessed | tf_op | source)
XLA Modules:
  0.0 53.2 jit_solution(13648852709466329657)
XLA Ops:
  0.6 3.0 %collective-permute-start = (bf16[16,8,128]{2,1,0:T(8,128)(2,1)}, bf16[16,8,128]{2,1,0:T(8,128)(2,1)S(1)}, u32[]{:S(2)}, u32[]{:S(2)}) collective-permute-start(bf16[16,8,128]{2,1,0:T(8,128)(2,1)} %refs_0_.1), channel_id=1, source_target_pairs={{0,1},{1,0},{2,3},{3,2},{4,5},{5,4},{6,7},{7,6},{8,9},{9,8},{10,11... | collective-permute-start | bytes 98312 | tf_op jit(solution)/shard_map/ppermute | solution.py:47
  3.7 1.5 %collective-permute-start.1 = (bf16[16,8,128]{2,1,0:T(8,128)(2,1)}, bf16[16,8,128]{2,1,0:T(8,128)(2,1)S(1)}, u32[]{:S(2)}, u32[]{:S(2)}) collective-permute-start(bf16[16,8,128]{2,1,0:T(8,128)(2,1)} %refs_0_.1), channel_id=1, source_target_pairs={{0,2},{1,3},{2,0},{3,1},{4,6},{5,7},{6,4},{7,5},{8,10},{9,11},{10,... | collective-permute-start | bytes 98312 | tf_op jit(solution)/shard_map/ppermute | solution.py:47
  5.2 0.0 collective-permute-start.2
  5.2 0.0 copy-start.2
  5.2 2.2 %copy-done.2 = bf16[16,256,2,2,128]{4,3,2,1,0:T(2,128)(2,1)S(1)} copy-done((bf16[16,256,2,2,128]{4,3,2,1,0:T(2,128)(2,1)S(1)}, bf16[16,256,2,2,128]{4,3,2,1,0:T(2,128)(2,1)}, u32[]{:S(2)}) %copy-start.2) | copy-done | bytes 4194328
  7.4 0.0 copy-start.5
  7.4 0.8 %copy-done.5 = bf16[16,8,128]{2,1,0:T(8,128)(2,1)S(1)} copy-done((bf16[16,8,128]{2,1,0:T(8,128)(2,1)S(1)}, bf16[16,8,128]{2,1,0:T(8,128)(2,1)}, u32[]{:S(2)}) %copy-start.5) | copy-done | bytes 32792
  8.2 0.0 copy-start.7
  8.2 0.7 %copy-done.7 = bf16[16,2,2,128]{3,2,1,0:T(2,128)(2,1)S(1)} copy-done((bf16[16,2,2,128]{3,2,1,0:T(2,128)(2,1)S(1)}, bf16[16,2,2,128]{3,2,1,0:T(2,128)(2,1)}, u32[]{:S(2)}) %copy-start.7) | copy-done | bytes 16408
  8.9 0.0 copy-start.9
  8.9 0.7 %copy-done.9 = s32[16]{0:T(128)S(1)} copy-done((s32[16]{0:T(128)S(1)}, s32[16]{0:T(128)}, u32[]{:S(2)}) %copy-start.9) | copy-done | bytes 88
  9.5 0.0 copy-start
  9.5 0.0 copy-start.1
  9.5 0.0 copy-start.6
  9.5 0.0 copy-start.3
  9.5 0.0 copy-start.8
  9.5 0.0 copy-start.10
  9.6 0.0 copy-start.11
  9.6 7.4 %cache_attention.1 = (bf16[128,128]{1,0:T(8,128)(2,1)S(1)}, f32[16,8,128]{2,1,0:T(8,128)S(1)}, f32[16,8,128]{2,1,0:T(8,128)S(1)}) custom-call(s32[16]{0:T(128)S(1)} %copy-done.9, bf16[16,8,128]{2,1,0:T(8,128)(2,1)S(1)} %copy-done.5, bf16[16,4,128]{2,1,0:T(4,128)(2,1)S(1)} %bitcast.6, bf16[16,1024,128]{2,1,0:T(8,128)(2,1)S(1)} %bitcast.5), custom_call_target="tpu_custom_call" | custom-call | flops 10000000000 | bytes 4194304 | tf_op jit(solution)/shard_map/cache_attention/pallas_call | solution.py:114
  17.0 0.0 collective-permute-done.refs_1_
  17.0 0.0 collective-permute-done.1.refs_2_
  17.0 0.0 collective-permute-done.2.refs_3_
  17.0 0.0 copy-done
  17.0 0.0 copy-done.1
  17.1 0.0 copy-done.6
  17.1 0.6 %make_table.1.refs_0_ = bf16[36,8,128]{2,1,0:T(8,128)(2,1)S(1)} custom-call(s32[4]{0:T(128)S(1)} %copy-done, s32[4]{0:T(128)S(1)} %copy-done.1, bf16[16,8,128]{2,1,0:T(8,128)(2,1)S(1)} %copy-done.6, bf16[16,8,128]{2,1,0:T(8,128)(2,1)S(1)} %collective-permute-done.refs_1_, bf16[16,8,128]{2,1,0:T(8,128)(2,1)S(1)} %collective-permute-done.1.refs_2_, ...), custom_call_target="tpu_custom_call" | custom-call | flops 100000000 | bytes 200000 | tf_op jit(solution)/shard_map/make_table/pallas_call | solution.py:267
  17.7 2.1 %collective-permute-start.3 = (bf16[36,8,128]{2,1,0:T(8,128)(2,1)S(1)}, bf16[36,8,128]{2,1,0:T(8,128)(2,1)S(1)}, u32[]{:S(2)}, u32[]{:S(2)}) collective-permute-start(bf16[36,8,128]{2,1,0:T(8,128)(2,1)S(1)} %make_table.1.refs_0_), channel_id=1, source_target_pairs={{0,4},{1,5},{2,6},{3,7},{4,0},{5,1},{6,2},{7,3},{8,12},{9,13},{10,... | collective-permute-start | bytes 221192 | tf_op jit(solution)/shard_map/ppermute | solution.py:47
  19.8 2.6 %collective-permute-start.4 = (bf16[36,8,128]{2,1,0:T(8,128)(2,1)S(1)}, bf16[36,8,128]{2,1,0:T(8,128)(2,1)S(1)}, u32[]{:S(2)}, u32[]{:S(2)}) collective-permute-start(bf16[36,8,128]{2,1,0:T(8,128)(2,1)S(1)} %make_table.1.refs_0_), channel_id=1, source_target_pairs={{0,8},{1,9},{2,10},{3,11},{4,12},{5,13},{6,14},{7,15},{8,0},{9,1},... | collective-permute-start | bytes 221192 | tf_op jit(solution)/shard_map/ppermute | solution.py:47
  22.4 0.0 collective-permute-start.5
  22.4 0.0 copy-done.3
  22.4 0.0 copy-done.8
  22.4 0.0 copy-done.10
  22.4 0.0 copy-done.11
  22.4 4.5 %project.1 = (bf16[2,256,128]{2,1,0:T(8,128)(2,1)S(1)}, bf16[2,256,128]{2,1,0:T(8,128)(2,1)S(1)}) custom-call(s32[4]{0:T(128)S(1)} %copy-done.10, bf16[256,4096]{1,0:T(8,128)(2,1)S(1)} %copy-done.3, f32[1,4096]{1,0:T(1,128)S(1)} %bitcast.7, f32[1,128]{1,0:T(1,128)S(1)} %copy-done.11, bf16[16384,128]{1,0:T(8,128)(2,1)} %bitcast.9), custom_call_target="tpu_custom_call" | custom-call | flops 10000000000 | bytes 6291456 | tf_op jit(solution)/shard_map/project/pallas_call | solution.py:206
  26.9 0.0 collective-permute-done.3.refs_1_
  26.9 0.0 collective-permute-done.4.refs_2_
  26.9 1.6 %collective-permute-done.5.refs_3_ = bf16[36,8,128]{2,1,0:T(8,128)(2,1)S(1)} collective-permute-done((bf16[36,8,128]{2,1,0:T(8,128)(2,1)S(1)}, bf16[36,8,128]{2,1,0:T(8,128)(2,1)S(1)}, u32[]{:S(2)}, u32[]{:S(2)}) %collective-permute-start.5) | collective-permute-done | bytes 73760 | tf_op jit(solution)/shard_map/ppermute | solution.py:47
  28.5 0.0 copy-start.4
  28.5 1.0 %prompt_attention.1.refs_0_ = bf16[688,128]{1,0:T(8,128)(2,1)S(1)} custom-call(s32[4]{0:T(128)S(1)} %copy-done.10, s32[4]{0:T(128)S(1)} %copy-done, s32[4]{0:T(128)S(1)} %copy-done.1, bf16[2,256,128]{2,1,0:T(8,128)(2,1)S(1)} %get-tuple-element.12.k_ref, bf16[2,256,128]{2,1,0:T(8,128)(2,1)S(1)} %get-tuple-element.13.v_ref, ...), custom_call_target="tpu_custom_call" | custom-call | flops 2000000000 | bytes 500000 | tf_op jit(solution)/shard_map/prompt_attention/pallas_call | solution.py:390
  29.5 1.6 %collective-permute-start.6 = (bf16[688,128]{1,0:T(8,128)(2,1)S(1)}, bf16[688,128]{1,0:T(8,128)(2,1)S(1)}, u32[]{:S(2)}, u32[]{:S(2)}) collective-permute-start(bf16[688,128]{1,0:T(8,128)(2,1)S(1)} %prompt_attention.1.refs_0_), channel_id=1, source_target_pairs={{0,1},{1,0},{2,3},{3,2},{4,5},{5,4},{6,7},{7,6},{8,9},{9,8},{10,11... | collective-permute-start | bytes 528392 | tf_op jit(solution)/shard_map/ppermute | solution.py:47
  31.1 1.5 %collective-permute-start.7 = (bf16[688,128]{1,0:T(8,128)(2,1)S(1)}, bf16[688,128]{1,0:T(8,128)(2,1)S(1)}, u32[]{:S(2)}, u32[]{:S(2)}) collective-permute-start(bf16[688,128]{1,0:T(8,128)(2,1)S(1)} %prompt_attention.1.refs_0_), channel_id=1, source_target_pairs={{0,2},{1,3},{2,0},{3,1},{4,6},{5,7},{6,4},{7,5},{8,10},{9,11},{10,... | collective-permute-start | bytes 528392 | tf_op jit(solution)/shard_map/ppermute | solution.py:47
  32.6 0.5 collective-permute-start.8
  33.1 2.9 %collective-permute-done.6.refs_1_ = bf16[688,128]{1,0:T(8,128)(2,1)S(1)} collective-permute-done((bf16[688,128]{1,0:T(8,128)(2,1)S(1)}, bf16[688,128]{1,0:T(8,128)(2,1)S(1)}, u32[]{:S(2)}, u32[]{:S(2)}) %collective-permute-start.6) | collective-permute-done | bytes 176160 | tf_op jit(solution)/shard_map/ppermute | solution.py:47
  35.9 1.7 %collective-permute-done.7.refs_2_ = bf16[688,128]{1,0:T(8,128)(2,1)S(1)} collective-permute-done((bf16[688,128]{1,0:T(8,128)(2,1)S(1)}, bf16[688,128]{1,0:T(8,128)(2,1)S(1)}, u32[]{:S(2)}, u32[]{:S(2)}) %collective-permute-start.7) | collective-permute-done | bytes 176160 | tf_op jit(solution)/shard_map/ppermute | solution.py:47
  37.6 1.4 %collective-permute-done.8.refs_3_ = bf16[688,128]{1,0:T(8,128)(2,1)S(1)} collective-permute-done((bf16[688,128]{1,0:T(8,128)(2,1)S(1)}, bf16[688,128]{1,0:T(8,128)(2,1)S(1)}, u32[]{:S(2)}, u32[]{:S(2)}) %collective-permute-start.8) | collective-permute-done | bytes 176160 | tf_op jit(solution)/shard_map/ppermute | solution.py:47
  39.0 0.4 merge_states.1.refs_0_
  39.4 0.1 collective-permute-start.9
  39.5 3.4 %collective-permute-start.10 = (bf16[176,128]{1,0:T(8,128)(2,1)S(1)}, bf16[176,128]{1,0:T(8,128)(2,1)S(1)}, u32[]{:S(2)}, u32[]{:S(2)}) collective-permute-start(bf16[176,128]{1,0:T(8,128)(2,1)S(1)} %merge_states.1.refs_0_), channel_id=1, source_target_pairs={{0,8},{1,9},{2,10},{3,11},{4,12},{5,13},{6,14},{7,15},{8,0},{9,1},... | collective-permute-start | bytes 135176 | tf_op jit(solution)/shard_map/ppermute | solution.py:47
  42.9 1.0 %collective-permute-start.11 = (bf16[176,128]{1,0:T(8,128)(2,1)S(1)}, bf16[176,128]{1,0:T(8,128)(2,1)S(1)}, u32[]{:S(2)}, u32[]{:S(2)}) collective-permute-start(bf16[176,128]{1,0:T(8,128)(2,1)S(1)} %merge_states.1.refs_0_), channel_id=1, source_target_pairs={{0,12},{1,13},{2,14},{3,15},{4,8},{5,9},{6,10},{7,11},{8,4},{9,5},... | collective-permute-start | bytes 135176 | tf_op jit(solution)/shard_map/ppermute | solution.py:47
  43.9 0.0 copy-done.4
  43.9 0.4 base_product.1
  44.3 0.1 collective-permute-start.12
  44.3 0.0 collective-permute-done.9.refs_1_
  44.3 0.8 %collective-permute-done.10.refs_2_ = bf16[176,128]{1,0:T(8,128)(2,1)S(1)} collective-permute-done((bf16[176,128]{1,0:T(8,128)(2,1)S(1)}, bf16[176,128]{1,0:T(8,128)(2,1)S(1)}, u32[]{:S(2)}, u32[]{:S(2)}) %collective-permute-start.10) | collective-permute-done | bytes 45088 | tf_op jit(solution)/shard_map/ppermute | solution.py:47
  45.2 3.6 %collective-permute-done.11.refs_3_ = bf16[176,128]{1,0:T(8,128)(2,1)S(1)} collective-permute-done((bf16[176,128]{1,0:T(8,128)(2,1)S(1)}, bf16[176,128]{1,0:T(8,128)(2,1)S(1)}, u32[]{:S(2)}, u32[]{:S(2)}) %collective-permute-start.11) | collective-permute-done | bytes 45088 | tf_op jit(solution)/shard_map/ppermute | solution.py:47
  48.7 1.8 %answer_product.1 = (bf16[16,8,128]{2,1,0:T(8,128)(2,1)}, f32[24,256]{1,0:T(8,128)S(1)}) custom-call(s32[4]{0:T(128)S(1)} %copy-done, s32[4]{0:T(128)S(1)} %copy-done.1, bf16[8,128,256]{2,1,0:T(8,128)(2,1)S(1)} %copy-done.4, f32[16,8,128]{2,1,0:T(8,128)S(1)} %get-tuple-element.11.o_ref, bf16[176,128]{1,0:T(8,128)(2,1)S(1)} %merge_states.1.refs_0_, ...), custom_call_target="tpu_custom_call" | custom-call | flops 1000000000 | bytes 1000000 | tf_op jit(solution)/shard_map/answer_product/pallas_call | solution.py:485
  50.5 0.0 collective-permute-start.13
  50.5 1.2 %collective-permute-done.13.part_taken = f32[24,256]{1,0:T(8,128)S(1)} collective-permute-done((f32[24,256]{1,0:T(8,128)S(1)}, f32[24,256]{1,0:T(8,128)S(1)}, u32[]{:S(2)}, u32[]{:S(2)}) %collective-permute-start.13) | collective-permute-done | bytes 24608 | tf_op jit(solution)/shard_map/ppermute | solution.py:529
  51.7 0.0 collective-permute-done.12.taken
  51.7 1.5 %finish.1 = bf16[128,256]{1,0:T(8,128)(2,1)} custom-call(s32[4]{0:T(128)S(1)} %copy-done, s32[4]{0:T(128)S(1)} %copy-done.1, f32[128,256]{1,0:T(8,128)S(1)} %get-tuple-element.17.keep, f32[128,256]{1,0:T(8,128)S(1)} %collective-permute-done.12.taken, f32[24,256]{1,0:T(8,128)S(1)} %get-tuple-element.19.part, f32[24,256]{1,0:T(8,128)S(1)} %collective-permute-done.13.part_taken), custom_call_target="tpu_custom_call" | custom-call | tf_op jit(solution)/shard_map/finish/pallas_call | solution.py:517
Async XLA Ops:
  0.6 16.4 %collective-permute-start = (bf16[16,8,128]{2,1,0:T(8,128)(2,1)}, bf16[16,8,128]{2,1,0:T(8,128)(2,1)S(1)}, u32[]{:S(2)}, u32[]{:S(2)}) collective-permute-start(bf16[16,8,128]{2,1,0:T(8,128)(2,1)} %refs_0_.1), channel_id=1, source_target_pairs={{0,1},{1,0},{2,3},{3,2},{4,5},{5,4},{6,7},{7,6},{8,9},{9,8},{10,11... | collective-permute-start | bytes 98312 | tf_op jit(solution)/shard_map/ppermute | solution.py:47
  3.7 13.3 %collective-permute-start.1 = (bf16[16,8,128]{2,1,0:T(8,128)(2,1)}, bf16[16,8,128]{2,1,0:T(8,128)(2,1)S(1)}, u32[]{:S(2)}, u32[]{:S(2)}) collective-permute-start(bf16[16,8,128]{2,1,0:T(8,128)(2,1)} %refs_0_.1), channel_id=1, source_target_pairs={{0,2},{1,3},{2,0},{3,1},{4,6},{5,7},{6,4},{7,5},{8,10},{9,11},{10,... | collective-permute-start | bytes 98312 | tf_op jit(solution)/shard_map/ppermute | solution.py:47
  5.2 11.8 %collective-permute-start.2 = (bf16[16,8,128]{2,1,0:T(8,128)(2,1)}, bf16[16,8,128]{2,1,0:T(8,128)(2,1)S(1)}, u32[]{:S(2)}, u32[]{:S(2)}) collective-permute-start(bf16[16,8,128]{2,1,0:T(8,128)(2,1)} %refs_0_.1), channel_id=1, source_target_pairs={{0,3},{1,2},{2,1},{3,0},{4,7},{5,6},{6,5},{7,4},{8,11},{9,10},{10,... | collective-permute-start | bytes 98312 | tf_op jit(solution)/shard_map/ppermute | solution.py:47
  5.2 2.2 %copy-start.2 = (bf16[16,256,2,2,128]{4,3,2,1,0:T(2,128)(2,1)S(1)}, bf16[16,256,2,2,128]{4,3,2,1,0:T(2,128)(2,1)}, u32[]{:S(2)}) copy-start(bf16[16,256,2,2,128]{4,3,2,1,0:T(2,128)(2,1)} %param.20) | copy-start | bytes 12582916
  7.4 0.8 %copy-start.5 = (bf16[16,8,128]{2,1,0:T(8,128)(2,1)S(1)}, bf16[16,8,128]{2,1,0:T(8,128)(2,1)}, u32[]{:S(2)}) copy-start(bf16[16,8,128]{2,1,0:T(8,128)(2,1)} %refs_0_.1) | copy-start | bytes 98308
  8.2 0.7 %copy-start.7 = (bf16[16,2,2,128]{3,2,1,0:T(2,128)(2,1)S(1)}, bf16[16,2,2,128]{3,2,1,0:T(2,128)(2,1)}, u32[]{:S(2)}) copy-start(bf16[16,2,2,128]{3,2,1,0:T(2,128)(2,1)} %param.19) | copy-start | bytes 49156
  8.9 0.7 %copy-start.9 = (s32[16]{0:T(128)S(1)}, s32[16]{0:T(128)}, u32[]{:S(2)}) copy-start(s32[16]{0:T(128)} %pos_ref.1) | copy-start | bytes 196
  9.5 7.5 %copy-start = (s32[4]{0:T(128)S(1)}, s32[4]{0:T(128)}, u32[]{:S(2)}) copy-start(s32[4]{0:T(128)} %owner.7) | copy-start | bytes 52
  9.5 7.5 %copy-start.1 = (s32[4]{0:T(128)S(1)}, s32[4]{0:T(128)}, u32[]{:S(2)}) copy-start(s32[4]{0:T(128)} %counts.7) | copy-start | bytes 52
  9.5 7.5 %copy-start.6 = (bf16[16,8,128]{2,1,0:T(8,128)(2,1)S(1)}, bf16[16,8,128]{2,1,0:T(8,128)(2,1)}, u32[]{:S(2)}) copy-start(bf16[16,8,128]{2,1,0:T(8,128)(2,1)} %refs_0_.1) | copy-start | bytes 98308
  9.5 12.8 %copy-start.3 = (bf16[256,4096]{1,0:T(8,128)(2,1)S(1)}, bf16[256,4096]{1,0:T(8,128)(2,1)}, u32[]{:S(2)}) copy-start(bf16[256,4096]{1,0:T(8,128)(2,1)} %hid_hbm.1) | copy-start | bytes 6291460
  9.5 12.8 %copy-start.8 = (f32[4096]{0:T(1024)S(1)}, f32[4096]{0:T(1024)}, u32[]{:S(2)}) copy-start(f32[4096]{0:T(1024)} %param.13) | copy-start | bytes 49156
  9.5 12.8 %copy-start.10 = (s32[4]{0:T(128)S(1)}, s32[4]{0:T(128)}, u32[]{:S(2)}) copy-start(s32[4]{0:T(128)} %excess.3) | copy-start | bytes 52
  9.6 12.8 %copy-start.11 = (f32[1,128]{1,0:T(1,128)S(1)}, f32[1,128]{1,0:T(1,128)}, u32[]{:S(2)}) copy-start(f32[1,128]{1,0:T(1,128)} %constant.2.clone.freq_ref) | copy-start | bytes 1540
  17.7 9.2 %collective-permute-start.3 = (bf16[36,8,128]{2,1,0:T(8,128)(2,1)S(1)}, bf16[36,8,128]{2,1,0:T(8,128)(2,1)S(1)}, u32[]{:S(2)}, u32[]{:S(2)}) collective-permute-start(bf16[36,8,128]{2,1,0:T(8,128)(2,1)S(1)} %make_table.1.refs_0_), channel_id=1, source_target_pairs={{0,4},{1,5},{2,6},{3,7},{4,0},{5,1},{6,2},{7,3},{8,12},{9,13},{10,... | collective-permute-start | bytes 221192 | tf_op jit(solution)/shard_map/ppermute | solution.py:47
  19.8 7.1 %collective-permute-start.4 = (bf16[36,8,128]{2,1,0:T(8,128)(2,1)S(1)}, bf16[36,8,128]{2,1,0:T(8,128)(2,1)S(1)}, u32[]{:S(2)}, u32[]{:S(2)}) collective-permute-start(bf16[36,8,128]{2,1,0:T(8,128)(2,1)S(1)} %make_table.1.refs_0_), channel_id=1, source_target_pairs={{0,8},{1,9},{2,10},{3,11},{4,12},{5,13},{6,14},{7,15},{8,0},{9,1},... | collective-permute-start | bytes 221192 | tf_op jit(solution)/shard_map/ppermute | solution.py:47
  22.4 6.2 %collective-permute-start.5 = (bf16[36,8,128]{2,1,0:T(8,128)(2,1)S(1)}, bf16[36,8,128]{2,1,0:T(8,128)(2,1)S(1)}, u32[]{:S(2)}, u32[]{:S(2)}) collective-permute-start(bf16[36,8,128]{2,1,0:T(8,128)(2,1)S(1)} %make_table.1.refs_0_), channel_id=1, source_target_pairs={{0,12},{1,13},{2,14},{3,15},{4,8},{5,9},{6,10},{7,11},{8,4},{9,5},... | collective-permute-start | bytes 221192 | tf_op jit(solution)/shard_map/ppermute | solution.py:47
  28.5 15.3 %copy-start.4 = (bf16[8,128,256]{2,1,0:T(8,128)(2,1)S(1)}, bf16[8,128,256]{2,1,0:T(8,128)(2,1)}, u32[]{:S(2)}) copy-start(bf16[8,128,256]{2,1,0:T(8,128)(2,1)} %w_ref.3) | copy-start | bytes 1572868
  29.5 6.4 %collective-permute-start.6 = (bf16[688,128]{1,0:T(8,128)(2,1)S(1)}, bf16[688,128]{1,0:T(8,128)(2,1)S(1)}, u32[]{:S(2)}, u32[]{:S(2)}) collective-permute-start(bf16[688,128]{1,0:T(8,128)(2,1)S(1)} %prompt_attention.1.refs_0_), channel_id=1, source_target_pairs={{0,1},{1,0},{2,3},{3,2},{4,5},{5,4},{6,7},{7,6},{8,9},{9,8},{10,11... | collective-permute-start | bytes 528392 | tf_op jit(solution)/shard_map/ppermute | solution.py:47
  31.1 6.6 %collective-permute-start.7 = (bf16[688,128]{1,0:T(8,128)(2,1)S(1)}, bf16[688,128]{1,0:T(8,128)(2,1)S(1)}, u32[]{:S(2)}, u32[]{:S(2)}) collective-permute-start(bf16[688,128]{1,0:T(8,128)(2,1)S(1)} %prompt_attention.1.refs_0_), channel_id=1, source_target_pairs={{0,2},{1,3},{2,0},{3,1},{4,6},{5,7},{6,4},{7,5},{8,10},{9,11},{10,... | collective-permute-start | bytes 528392 | tf_op jit(solution)/shard_map/ppermute | solution.py:47
  32.6 6.4 %collective-permute-start.8 = (bf16[688,128]{1,0:T(8,128)(2,1)S(1)}, bf16[688,128]{1,0:T(8,128)(2,1)S(1)}, u32[]{:S(2)}, u32[]{:S(2)}) collective-permute-start(bf16[688,128]{1,0:T(8,128)(2,1)S(1)} %prompt_attention.1.refs_0_), channel_id=1, source_target_pairs={{0,3},{1,2},{2,1},{3,0},{4,7},{5,6},{6,5},{7,4},{8,11},{9,10},{10,... | collective-permute-start | bytes 528392 | tf_op jit(solution)/shard_map/ppermute | solution.py:47
  39.4 4.9 %collective-permute-start.9 = (bf16[176,128]{1,0:T(8,128)(2,1)S(1)}, bf16[176,128]{1,0:T(8,128)(2,1)S(1)}, u32[]{:S(2)}, u32[]{:S(2)}) collective-permute-start(bf16[176,128]{1,0:T(8,128)(2,1)S(1)} %merge_states.1.refs_0_), channel_id=1, source_target_pairs={{0,4},{1,5},{2,6},{3,7},{4,0},{5,1},{6,2},{7,3},{8,12},{9,13},{10,... | collective-permute-start | bytes 135176 | tf_op jit(solution)/shard_map/ppermute | solution.py:47
  39.5 5.7 %collective-permute-start.10 = (bf16[176,128]{1,0:T(8,128)(2,1)S(1)}, bf16[176,128]{1,0:T(8,128)(2,1)S(1)}, u32[]{:S(2)}, u32[]{:S(2)}) collective-permute-start(bf16[176,128]{1,0:T(8,128)(2,1)S(1)} %merge_states.1.refs_0_), channel_id=1, source_target_pairs={{0,8},{1,9},{2,10},{3,11},{4,12},{5,13},{6,14},{7,15},{8,0},{9,1},... | collective-permute-start | bytes 135176 | tf_op jit(solution)/shard_map/ppermute | solution.py:47
  42.9 5.8 %collective-permute-start.11 = (bf16[176,128]{1,0:T(8,128)(2,1)S(1)}, bf16[176,128]{1,0:T(8,128)(2,1)S(1)}, u32[]{:S(2)}, u32[]{:S(2)}) collective-permute-start(bf16[176,128]{1,0:T(8,128)(2,1)S(1)} %merge_states.1.refs_0_), channel_id=1, source_target_pairs={{0,12},{1,13},{2,14},{3,15},{4,8},{5,9},{6,10},{7,11},{8,4},{9,5},... | collective-permute-start | bytes 135176 | tf_op jit(solution)/shard_map/ppermute | solution.py:47
  44.3 7.5 %collective-permute-start.12 = (f32[128,256]{1,0:T(8,128)S(1)}, f32[128,256]{1,0:T(8,128)S(1)}, u32[]{:S(2)}, u32[]{:S(2)}) collective-permute-start(f32[128,256]{1,0:T(8,128)S(1)} %get-tuple-element.18), channel_id=1, source_target_pairs={{0,16},{16,0},{1,17},{17,1},{2,18},{18,2},{3,19},{19,3},{4,20},{20... | collective-permute-start | bytes 393224 | tf_op jit(solution)/shard_map/ppermute | solution.py:529
  50.5 1.2 %collective-permute-start.13 = (f32[24,256]{1,0:T(8,128)S(1)}, f32[24,256]{1,0:T(8,128)S(1)}, u32[]{:S(2)}, u32[]{:S(2)}) collective-permute-start(f32[24,256]{1,0:T(8,128)S(1)} %get-tuple-element.19.part), channel_id=1, source_target_pairs={{0,16},{16,0},{1,17},{17,1},{2,18},{18,2},{3,19},{19,3},{4,20},{20... | collective-permute-start | bytes 73736 | tf_op jit(solution)/shard_map/ppermute | solution.py:529

commit v2 on v1

--- a/solution.py
+++ b/solution.py
@@ -14,10 +14,12 @@
 EPS = 1e-05
 LOW = -1e30
 LANES = 128
+CACHE_MIB = 24
+CACHE_BLOCKS = 4
 
 SMEM = pl.BlockSpec(memory_space=pltpu.SMEM)
 VMEM = pl.BlockSpec(memory_space=pltpu.VMEM)
-ANY = pl.BlockSpec(memory_space=pl.ANY)
+HBM = pl.BlockSpec(memory_space=pltpu.HBM)
 NT = (((1,), (1,)), ((), ()))
 NN = (((1,), (0,)), ((), ()))
 
@@ -26,8 +28,12 @@
     return pl.CostEstimate(flops=flops, bytes_accessed=bytes_accessed, transcendentals=0)
 
 
-def params(mib=48):
+def params(mib=24):
     return pltpu.CompilerParams(vmem_limit_bytes=mib << 20)
+
+
+def in_hbm(x):
+    return pltpu.with_memory_space_constraint(x, pltpu.HBM)
 
 
 def phases(n):
@@ -64,93 +70,137 @@
     return lax.rem(lax.div(index, stride), radix)
 
 
-def cache_kernel(per, pos_ref, q_ref, new_ref, cache_ref, out_ref, o_ref, lse_ref, att):
-    slots, heads, size = q_ref.shape
-    ways = new_ref.shape[1]
+def cache_kernel(
+    pos_hbm, q_hbm, new_hbm, cache_hbm, hid_hbm, out_ref, o_ref, lse_ref, hid,
+    att, table, key, value, pos, qs, fresh, cache, small, sems,
+):
+    slots, heads, size = qs.shape
+    ways = fresh.shape[1]
     group = heads // (ways // 2)
-    rows = cache_ref.shape[1]
+    rows = cache.shape[1]
     scale = size ** (-0.5)
-    step = pl.program_id(0)
+    blocks = sems.shape[0]
+    block = slots // blocks
+    first = [
+        pltpu.make_async_copy(pos_hbm, pos, small.at[0]),
+        pltpu.make_async_copy(q_hbm, qs, small.at[1]),
+        pltpu.make_async_copy(new_hbm, fresh, small.at[2]),
+    ]
+    for load in first:
+        load.start()
+    loads = []
+    for i in range(blocks):
+        part = pl.ds(i * block, block)
+        loads.append(pltpu.make_async_copy(cache_hbm.at[part], cache.at[part], sems.at[i]))
+        loads[-1].start()
+    extra = pltpu.make_async_copy(hid_hbm, hid, small.at[3])
+    extra.start()
+    for load in first:
+        load.wait()
     head = lax.broadcasted_iota(jnp.int32, (heads, 1), 0) // group
-    column = lax.broadcasted_iota(jnp.int32, (heads, rows), 1)
-    mine = (column % ways) == 2 * head
-    for i in range(per):
-        s = step * per + i
-        q = q_ref[s]
-        scores = dot(q, cache_ref[i], NT) * scale
-        valid = mine & (column < pos_ref[s] * ways)
-        scores = jnp.where(valid, scores, LOW)
-        fresh = new_ref[s].astype(jnp.float32)
-        key = jnp.zeros((heads, size), jnp.float32)
-        value = jnp.zeros((heads, size), jnp.float32)
+    for s in range(slots):
+        new = fresh[s].astype(jnp.float32)
+        k = jnp.zeros((heads, size), jnp.float32)
+        v = jnp.zeros((heads, size), jnp.float32)
         for n in range(ways // 2):
-            key = jnp.where(head == n, fresh[2 * n : 2 * n + 1, :], key)
-            value = jnp.where(head == n, fresh[2 * n + 1 : 2 * n + 2, :], value)
-        own = jnp.sum(q.astype(jnp.float32) * key, axis=1, keepdims=True) * scale
+            k = jnp.where(head == n, new[2 * n : 2 * n + 1, :], k)
+            v = jnp.where(head == n, new[2 * n + 1 : 2 * n + 2, :], v)
+        key[s * heads : (s + 1) * heads, :] = qs[s].astype(jnp.float32) * k
+        value[s * heads : (s + 1) * heads, :] = v
+    line = lax.broadcasted_iota(jnp.int32, (block * heads, 1), 0)
+    column = lax.broadcasted_iota(jnp.int32, (block * heads, rows), 1)
+    mine = jnp.where((column % ways) == 2 * ((line % heads) // group), column, rows * ways)
+
+    def score(i):
+        for s in range(i * block, (i + 1) * block):
+            table[s * heads : (s + 1) * heads, :] = dot(qs[s], cache[s], NT)
+
+    def weigh(i):
+        at = slice(i * block * heads, (i + 1) * block * heads)
+        limit = jnp.zeros((block * heads, 1), jnp.int32)
+        for j in range(block):
+            limit = jnp.where(line // heads == j, pos[i * block + j] * ways, limit)
+        valid = mine < limit
+        scores = jnp.where(valid, table[at, :] * scale, LOW)
+        own = jnp.sum(key[at, :], axis=1, keepdims=True) * scale
         peak = jnp.maximum(jnp.max(scores, axis=1, keepdims=True), own)
         weights = jnp.where(valid, jnp.exp(scores - peak), 0.0)
         alone = jnp.exp(own - peak)
         total = jnp.sum(weights, axis=1, keepdims=True) + alone
-        moved = pltpu.roll(weights, 1, axis=1).astype(jnp.bfloat16)
-        mixed = dot(moved, cache_ref[i], NN)
-        mixed = mixed + alone.astype(jnp.bfloat16).astype(jnp.float32) * value
-        mixed = mixed / total
-        o_ref[s] = mixed
-        lse_ref[s] = jnp.broadcast_to(peak + jnp.log(total), (heads, size))
-        att[pl.ds(s, heads, stride=slots), :] = mixed
-
-    @pl.when(step == pl.num_programs(0) - 1)
-    def _():
-        out_ref[...] = att[...].astype(out_ref.dtype)
-
-
-def cache_attention(positions, queries, new_kv, response_cache):
+        table[at, :] = pltpu.roll(weights, 1, axis=1)
+        return peak + jnp.log(total), alone.astype(jnp.bfloat16).astype(jnp.float32), total
+
+    def mix(i, stats):
+        for j in range(block):
+            s = i * block + j
+            at = slice(s * heads, (s + 1) * heads)
+            mixed = dot(table[at, :].astype(jnp.bfloat16), cache[s], NN)
+            lse, alone, total = (x[j * heads : (j + 1) * heads] for x in stats)
+            mixed = (mixed + alone * value[at, :]) / total
+            o_ref[s] = mixed
+            lse_ref[s] = jnp.broadcast_to(lse, (heads, size))
+            att[pl.ds(s, heads, stride=slots), :] = mixed
+
+    stats = {}
+    for i in range(blocks + 2):
+        if i < blocks:
+            loads[i].wait()
+            score(i)
+        if 0 <= i - 1 < blocks:
+            stats[i - 1] = weigh(i - 1)
+        if 0 <= i - 2:
+            mix(i - 2, stats[i - 2])
+    out_ref[...] = att[...].astype(out_ref.dtype)
+    extra.wait()
+
+
+def cache_attention(positions, queries, new_kv, response_cache, prompt_hidden):
     slots, heads, size = queries.shape
     ctx, kv = response_cache.shape[1], response_cache.shape[2]
     rows = ctx * kv * 2
-    per = 2
-    whole = lambda *shape: pl.BlockSpec(shape, lambda i: (0,) * len(shape))
-    f32 = jnp.float32
-    return pl.pallas_call(
-        functools.partial(cache_kernel, per),
-        grid=(slots // per,),
-        in_specs=[
-            SMEM,
-            whole(slots, heads, size),
-            whole(slots, kv * 2, size),
-            pl.BlockSpec((per, rows, size), lambda i: (i, 0, 0)),
-        ],
-        out_specs=[
-            whole(slots * heads, size),
-            whole(slots, heads, size),
-            whole(slots, heads, size),
-        ],
+    blocks = CACHE_BLOCKS if slots % CACHE_BLOCKS == 0 else 1
+    f32, bf16 = jnp.float32, jnp.bfloat16
+    return pl.pallas_call(
+        cache_kernel,
+        in_specs=[HBM] * 5,
+        out_specs=[VMEM] * 4,
         out_shape=[
-            jax.ShapeDtypeStruct((slots * heads, size), jnp.bfloat16),
+            jax.ShapeDtypeStruct((slots * heads, size), bf16),
             jax.ShapeDtypeStruct((slots, heads, size), f32),
             jax.ShapeDtypeStruct((slots, heads, size), f32),
+            jax.ShapeDtypeStruct(prompt_hidden.shape, bf16),
         ],
-        scratch_shapes=[pltpu.VMEM((slots * heads, size), f32)],
-        compiler_params=params(),
+        scratch_shapes=[
+            pltpu.VMEM((slots * heads, size), f32),
+            pltpu.VMEM((slots * heads, rows), f32),
+            pltpu.VMEM((slots * heads, size), f32),
+            pltpu.VMEM((slots * heads, size), f32),
+            pltpu.SMEM((slots,), jnp.int32),
+            pltpu.VMEM((slots, heads, size), bf16),
+            pltpu.VMEM((slots, kv * 2, size), bf16),
+            pltpu.VMEM((slots, rows, size), bf16),
+            pltpu.SemaphoreType.DMA((4,)),
+            pltpu.SemaphoreType.DMA((blocks,)),
+        ],
+        compiler_params=params(CACHE_MIB),
         cost_estimate=cost(10_000_000_000, slots * rows * size * 2),
         name="cache_attention",
     )(
-        positions,
-        queries,
-        new_kv.reshape(slots, kv * 2, size),
-        response_cache.reshape(slots, rows, size),
+        in_hbm(positions),
+        in_hbm(queries),
+        in_hbm(new_kv.reshape(slots, kv * 2, size)),
+        in_hbm(response_cache.reshape(slots, rows, size)),
+        in_hbm(prompt_hidden),
     )
 
 
 def project_kernel(
-    chunks, excess, hid_hbm, gain_ref, freq_ref, w_hbm, k_ref, v_ref, hid, w, wide, acc, hsem, wsem
+    chunks, excess, hid, gain_ref, freq_ref, w_hbm, k_ref, v_ref, w, wide, acc, turn, wsem
 ):
     rows, width = hid.shape
     size = w.shape[1]
     ways = w.shape[0] // width
     depth = width // chunks
-    load = pltpu.make_async_copy(hid_hbm, hid, hsem)
-    load.start()
     loads = []
     for c in range(chunks):
         part = pl.ds(c * depth * ways, depth * ways)
@@ -161,11 +211,9 @@
     for p in range(excess.shape[0]):
         offset = jnp.where(token >= start, token - start, offset)
         start = start + PROMPT_MIN + excess[p]
+    lane = lax.broadcasted_iota(jnp.int32, (rows, size), 1)
     angle = offset.astype(jnp.float32) * freq_ref[...]
-    lane = lax.broadcasted_iota(jnp.int32, (rows, size), 1)
-    cosine = jnp.cos(angle)
-    sine = jnp.where(lane < size // 2, -1.0, 1.0) * jnp.sin(angle)
-    load.wait()
+    turn[...] = jnp.cos(jnp.where(lane < size // 2, angle, angle - np.float32(np.pi / 2)))
     total = jnp.zeros((rows, 1), jnp.float32)
     for c in range(chunks):
         x = hid[:, c * depth : (c + 1) * depth].astype(jnp.float32)
@@ -186,6 +234,11 @@
             acc[...] = term
         else:
             acc[...] += term
+    first = lane < size // 2
+    both = turn[...]
+    swapped = pltpu.roll(both, size // 2, axis=1)
+    cosine = jnp.where(first, both, swapped)
+    sine = jnp.where(first, -swapped, both)
     for n in range(ways // 2):
         key = acc[:, 2 * n * size : (2 * n + 1) * size]
         turned = key * cosine + pltpu.roll(key, size // 2, axis=1) * sine
@@ -205,15 +258,14 @@
     f32, bf16 = jnp.float32, jnp.bfloat16
     return pl.pallas_call(
         functools.partial(project_kernel, chunks),
-        in_specs=[SMEM, ANY, VMEM, VMEM, ANY],
+        in_specs=[SMEM, VMEM, VMEM, VMEM, HBM],
         out_specs=[VMEM, VMEM],
         out_shape=[jax.ShapeDtypeStruct((kv, rows, size), bf16)] * 2,
         scratch_shapes=[
-            pltpu.VMEM((rows, width), bf16),
             pltpu.VMEM((width * ways, size), bf16),
             pltpu.VMEM((2, depth * ways, size), f32),
             pltpu.VMEM((rows, ways * size), f32),
-            pltpu.SemaphoreType.DMA,
+            pltpu.VMEM((rows, size), f32),
             pltpu.SemaphoreType.DMA((chunks,)),
         ],
         compiler_params=params(),
@@ -224,7 +276,7 @@
         prompt_hidden,
         norm_gain[None, :],
         freq,
-        kv_weight.reshape(width * ways, size),
+        in_hbm(kv_weight.reshape(width * ways, size)),
     )
 
 
@@ -326,10 +378,10 @@
 
 
 def prompt_kernel(
-    phase, raw, carried, excess, owner, counts, k_ref, v_ref, o_ref, lse_ref, *refs
+    phase, carried, excess, owner, counts, k_ref, v_ref, o_ref, lse_ref, *refs
 ):
     radix = phase[1]
-    sources, out, table, mine_o, mine_lse = refs[:radix], refs[-4], refs[-3], refs[-2], refs[-1]
+    sources, out, pay, table, mine_o, mine_lse = refs[:radix], *refs[radix:]
     kv, tokens, size = k_ref.shape
     slots, heads, _ = o_ref.shape
     group = heads // kv
@@ -341,7 +393,7 @@
         for r in range(RESP):
             t = p * RESP + r
             slot = slot_of(owner, counts, p, r, slots)
-            tile = pick_tile(sources, owner[p], phase, slot if raw else t)
+            tile = pick_tile(sources, owner[p], phase, t)
             table[t * heads : (t + 1) * heads, :] = tile.astype(jnp.float32)
             mine_o[t * heads : (t + 1) * heads, :] = o_ref[slot]
             mine_lse[t * heads : (t + 1) * heads, :] = jnp.where(here, lse_ref[slot], LOW)
@@ -374,24 +426,23 @@
     total = total * left + right
     mixed = (mixed * left + mine_o[...] * right) / total
     put_state(out, mixed, top + jnp.log(total), rows)
-    at = rows + stat_rows(rows)
     entries = prompts * RESP
-    for source in sources:
-        block = source[entries : entries + carried] if not raw else source[...]
-        out[at : at + carried * heads, :] = block.reshape(carried * heads, size)
-        at += carried * heads
+    for i, source in enumerate(sources):
+        pay[i * carried : (i + 1) * carried] = source[entries : entries + carried]
 
 
 def prompt_attention(phase, carried, excess, owner, counts, keys, values, o, lse, sources):
     heads, size = o.shape[1:]
     rows = owner.shape[0] * RESP * heads
-    total = rows + stat_rows(rows) + carried * heads * len(sources)
     f32 = jnp.float32
     return pl.pallas_call(
-        functools.partial(prompt_kernel, phase, False, carried),
+        functools.partial(prompt_kernel, phase, carried),
         in_specs=[SMEM] * 3 + [VMEM] * (4 + len(sources)),
-        out_specs=VMEM,
-        out_shape=jax.ShapeDtypeStruct((total, size), jnp.bfloat16),
+        out_specs=[VMEM, VMEM],
+        out_shape=[
+            jax.ShapeDtypeStruct((rows + stat_rows(rows), size), jnp.bfloat16),
+            jax.ShapeDtypeStruct((carried * len(sources), heads, size), jnp.bfloat16),
+        ],
         scratch_shapes=[pltpu.VMEM((rows, size), f32)] * 3,
         compiler_params=params(),
         cost_estimate=cost(2_000_000_000, 500_000),
@@ -417,15 +468,15 @@
     )(*messages)
 
 
-def base_kernel(offsets, skip, slots, w_ref, *refs):
-    sources, keep, give, lhs = refs[:-3], refs[-3], refs[-2], refs[-1]
+def base_kernel(offsets, slots, owner, counts, w_ref, *refs):
+    sources, keep, give, pick, lhs = refs[:-4], *refs[-4:]
     heads, size, _ = w_ref.shape
     me = lax.axis_index("dev")
     block = slots * heads
     per = len(offsets) // len(sources)
     for i, offset in enumerate(offsets):
         at = pl.multiple_of(jnp.bitwise_xor(me, offset) * slots, slots)
-        begin = skip + (i % per) * block
+        begin = (i % per) * block
         for h in range(heads):
             lhs[pl.ds(at, slots), h * size : (h + 1) * size] = sources[i // per][
                 begin + h * slots : begin + (h + 1) * slots, :
@@ -435,94 +486,110 @@
     weight = w_ref[...].reshape(heads * size, w_ref.shape[2])
     keep[...] = dot(lhs[pl.ds(pl.multiple_of(role * half, half), half), :], weight, NN)
     give[...] = dot(lhs[pl.ds(pl.multiple_of((1 - role) * half, half), half), :], weight, NN)
-
-
-def base_product(offsets, skip, slots, weight, sources):
+    entry = lax.broadcasted_iota(jnp.int32, (1, pick.shape[1]), 1)
+    row = jnp.full((1, pick.shape[1]), -1, jnp.int32)
+    for p in range(owner.shape[0]):
+        start = owner[p] * slots + first_slot(owner, counts, p) - role * half
+        rank = entry - p * RESP
+        live = (rank >= 0) & (rank < RESP) & (rank < counts[p])
+        row = jnp.where(live, start + rank, row)
+    line = lax.broadcasted_iota(jnp.int32, pick.shape, 0)
+    pick[...] = jnp.where(line == row, 1.0, 0.0)
+
+
+def base_product(offsets, slots, entries, owner, counts, weight, sources):
     heads, size, columns = weight.shape
     total = len(offsets) * slots
     half = jax.ShapeDtypeStruct((total // 2, columns), jnp.float32)
     return pl.pallas_call(
-        functools.partial(base_kernel, offsets, skip, slots),
-        in_specs=[VMEM] * (1 + len(sources)),
-        out_specs=[VMEM, VMEM],
-        out_shape=[half, half],
+        functools.partial(base_kernel, offsets, slots),
+        in_specs=[SMEM, SMEM] + [VMEM] * (1 + len(sources)),
+        out_specs=[VMEM] * 3,
+        out_shape=[half, half, jax.ShapeDtypeStruct((total // 2, entries), jnp.float32)],
         scratch_shapes=[pltpu.VMEM((total, heads * size), jnp.bfloat16)],
         compiler_params=params(),
         cost_estimate=cost(2_000_000_000, 1_000_000),
         name="base_product",
-    )(weight, *sources)
-
-
-def answer_kernel(rows, owner, counts, w_ref, o_ref, *refs):
-    messages, att_ref, part, joined = refs[:-3], refs[-3], refs[-2], refs[-1]
-    heads, size, columns = w_ref.shape
-    slots = o_ref.shape[0]
-    entries = rows // heads
+    )(owner, counts, weight, *sources)
+
+
+def answer_kernel(rows, w_ref, *refs):
+    messages, answers, part, joined = refs[:-3], *refs[-3:]
+    heads = w_ref.shape[0]
     mixed, _ = merge(messages, rows)
     joined[...] = mixed
-    att_ref[...] = o_ref[...].astype(att_ref.dtype)
+    answers[...] = mixed.astype(answers.dtype)
+    total = None
+    for h in range(heads):
+        lhs = joined[pl.ds(h, rows // heads, stride=heads), :].astype(jnp.bfloat16)
+        term = dot(lhs, w_ref[h], NN)
+        total = term if total is None else total + term
+    part[: rows // heads, :] = total
+    rest = part.shape[0] - rows // heads
+    if rest:
+        part[rows // heads :, :] = jnp.zeros((rest, part.shape[1]), part.dtype)
+
+
+def answer_product(rows, entries, weight, messages):
+    heads, size, columns = weight.shape
+    return pl.pallas_call(
+        functools.partial(answer_kernel, rows),
+        in_specs=[VMEM] * (1 + len(messages)),
+        out_specs=[VMEM, VMEM],
+        out_shape=[
+            jax.ShapeDtypeStruct((rows, size), jnp.bfloat16),
+            jax.ShapeDtypeStruct((entries, columns), jnp.float32),
+        ],
+        scratch_shapes=[pltpu.VMEM((rows, size), jnp.float32)],
+        compiler_params=params(),
+        cost_estimate=cost(1_000_000_000, 1_000_000),
+        name="answer_product",
+    )(weight, *messages)
+
+
+def attended_kernel(owner, counts, o_ref, answers, out):
+    slots = o_ref.shape[0]
+    out[...] = o_ref[...].astype(out.dtype)
     me = lax.axis_index("dev")
     for p in range(owner.shape[0]):
         for r in range(RESP):
-            t = p * RESP + r
 
             @pl.when((owner[p] == me) & (r < counts[p]))
             def _():
-                tile = joined[t * heads : (t + 1) * heads, :]
-                att_ref[slot_of(owner, counts, p, r, slots)] = tile.astype(att_ref.dtype)
-
-    total = None
-    for h in range(heads):
-        lhs = joined[pl.ds(h, entries, stride=heads), :].astype(jnp.bfloat16)
-        term = dot(lhs, w_ref[h], NN)
-        total = term if total is None else total + term
-    part[:entries, :] = total
-
-
-def answer_product(rows, owner, counts, weight, o, messages):
-    heads, size, columns = weight.shape
-    entries = rows // heads
-    return pl.pallas_call(
-        functools.partial(answer_kernel, rows),
-        in_specs=[SMEM, SMEM] + [VMEM] * (2 + len(messages)),
-        out_specs=[VMEM, VMEM],
-        out_shape=[
-            jax.ShapeDtypeStruct(o.shape, jnp.bfloat16),
-            jax.ShapeDtypeStruct((8 * pl.cdiv(entries, 8), columns), jnp.float32),
-        ],
-        scratch_shapes=[pltpu.VMEM((rows, size), jnp.float32)],
-        compiler_params=params(),
-        cost_estimate=cost(1_000_000_000, 1_000_000),
-        name="answer_product",
-    )(owner, counts, weight, o, *messages)
-
-
-def finish_kernel(slots, owner, counts, keep, taken, part, part_taken, out, wide):
-    half = keep.shape[0]
-    begin = lax.axis_index("role") * half
-    wide[...] = keep[...] + taken[...]
-    for p in range(owner.shape[0]):
-        for r in range(RESP):
-            t = p * RESP + r
-            row = owner[p] * slots + slot_of(owner, counts, p, r, slots) - begin
-
-            @pl.when((r < counts[p]) & (row >= 0) & (row < half))
-            def _():
-                wide[pl.ds(row, 1), :] = part[t : t + 1, :] + part_taken[t : t + 1, :]
-
-    out[...] = wide[...].astype(out.dtype)
-
-
-def finish(slots, owner, counts, keep, taken, part, part_taken):
-    return pl.pallas_call(
-        functools.partial(finish_kernel, slots),
-        in_specs=[SMEM, SMEM] + [VMEM] * 4,
+                out[slot_of(owner, counts, p, r, slots)] = answers[p * RESP + r]
+
+
+def attended_rows(owner, counts, o, answers):
+    return pl.pallas_call(
+        attended_kernel,
+        in_specs=[SMEM, SMEM, VMEM, VMEM],
+        out_specs=VMEM,
+        out_shape=jax.ShapeDtypeStruct(o.shape, jnp.bfloat16),
+        compiler_params=params(),
+        cost_estimate=cost(500_000_000, 1_000_000),
+        name="attended_rows",
+    )(owner, counts, o, answers)
+
+
+def finish_kernel(keep, taken, part, part_taken, pick, out):
+    chosen = pick[...]
+    fixed = part[...] + part_taken[...]
+    patch = lax.dot_general(
+        chosen, fixed, NN, precision=lax.Precision.HIGHEST, preferred_element_type=jnp.float32
+    )
+    answered = jnp.max(chosen, axis=1, keepdims=True) > 0.5
+    out[...] = jnp.where(answered, patch, keep[...] + taken[...]).astype(out.dtype)
+
+
+def finish(keep, taken, part, part_taken, pick):
+    return pl.pallas_call(
+        finish_kernel,
+        in_specs=[VMEM] * 5,
         out_specs=VMEM,
         out_shape=jax.ShapeDtypeStruct(keep.shape, jnp.bfloat16),
-        scratch_shapes=[pltpu.VMEM(keep.shape, jnp.float32)],
         compiler_params=params(),
         name="finish",
-    )(owner, counts, keep, taken, part, part_taken)
+    )(keep, taken, part, part_taken, pick)
 
 
 def swap_role(x):
@@ -546,7 +613,9 @@
     steps = phases(lax.axis_size("dev"))
     rows = owner.shape[0] * RESP * heads
     received = [queries] + exchange(queries, steps[0])
-    local, o, lse = cache_attention(positions, queries, new_kv, response_cache)
+    local, o, lse, hidden = cache_attention(
+        positions, queries, new_kv, response_cache, prompt_hidden
+    )
     local = local.reshape(slots, heads, size)
     offsets = [0]
     carried = slots
@@ -557,20 +626,24 @@
         carried = carried if raw else carried * before[1]
         offsets = [k * phase[0] ^ a for k in range(phase[1]) for a in offsets]
         raw = False
-    keys, values = project(prompt_hidden, norm_gain, kv_weight, excess)
-    message = prompt_attention(
+    keys, values = project(hidden, norm_gain, kv_weight, excess)
+    message, payload = prompt_attention(
         steps[-1], carried, excess, owner, counts, keys, values, o, lse, received
     )
+    payload = payload.reshape(-1, size)
     received = [message] + exchange(message, steps[0])
+    blocks = [payload] + exchange(payload, steps[0])
     offsets = [k * steps[0][0] ^ a for k in range(steps[0][1]) for a in offsets]
-    blocks = received
     for phase in steps[1:]:
         message = merge_states(rows, received)
         received = [message] + exchange(message, phase)
-    keep, give = base_product(offsets, rows + stat_rows(rows), slots, out_weight, blocks)
+    entries = 8 * pl.cdiv(rows // heads, 8)
+    keep, give, pick = base_product(offsets, slots, entries, owner, counts, out_weight, blocks)
     taken = swap_role(give)
-    attended, part = answer_product(rows, owner, counts, out_weight, o, received)
-    block_out = finish(slots, owner, counts, keep, taken, part, swap_role(part))
+    answers, part = answer_product(rows, entries, out_weight, received)
+    part_taken = swap_role(part)
+    attended = attended_rows(owner, counts, o, answers.reshape(-1, heads, size))
+    block_out = finish(keep, taken, part, part_taken, pick)
     return (attended, block_out)
 
 

time: 53.5 us -> 41.8 us (0.78)
  waiting for transfers between devices: 13.1 us -> 6.57 us
  local copies, waits for them, and re-layouts: 4.35 us -> 0.03 us
  Pallas kernels: 17.6 us -> 13.7 us
  starting transfers between devices: 17.3 us -> 20.6 us
    ppermute x12 -> x15, waiting for transfers between devices: 11.9 us -> 6.57 us  [exchange(): lax.ppermute(x, 'dev', [(i, i ^ k * stride) for i in range(n)])]
    unnamed x24 -> x14, local copies, waits for them, and re-layouts: 4.35 us -> 0.03 us
    pallas_call x5 -> x6, Pallas kernels: 12.1 us -> 8.35 us  [the longest x1 3.67 us: cache_attention(): pl.pallas_call(cache_kernel, in_specs=[HBM] * 5, out_specs=[VMEM] * 4, ou...]
    ppermute x12 -> x15, starting transfers between devices: 17.3 us -> 20.5 us  [exchange(): lax.ppermute(x, 'dev', [(i, i ^ k * stride) for i in range(n)])]
    ppermute x2, waiting for transfers between devices: 1.2 us -> 0.01 us  [swap_role(): return lax.ppermute(x, 'role', [(0, 1), (1, 0)])]
  transfers between devices with their start and end apart: 14 -> 17, of which waited for: 7 -> 4; matrix products, arithmetic and copies ran while one was open for 0% -> 0% of each run, Pallas kernels for 27% -> 27%
where the time goes in v2:
time: 41.8 us; the launch traced here: 41.7 us
  starting transfers between devices  20.6 us (49%)
  Pallas kernels  13.7 us (33%)
  waiting for transfers between devices  6.57 us (16%)
  between operations  0.79 us (2%)
    ppermute x15, starting transfers between devices, exchange(): lax.ppermute(x, 'dev', [(i, i ^ k * stride) for i in range(n)])  20.5 us
    ppermute x15, waiting for transfers between devices, exchange(): lax.ppermute(x, 'dev', [(i, i ^ k * stride) for i in range(n)])  6.57 us
    pallas_call x1, Pallas kernels, project(): pl.pallas_call(functools.partial(project_kernel, chunks), in_specs=[SMEM,...  4.33 us
    pallas_call x1, Pallas kernels, cache_attention(): pl.pallas_call(cache_kernel, in_specs=[HBM] * 5, out_specs=[VMEM] * 4, ou...  3.67 us
    pallas_call x1, Pallas kernels, attended_rows(): pl.pallas_call(attended_kernel, in_specs=[SMEM, SMEM, VMEM, VMEM], out_sp...  1.36 us
    pallas_call x1, Pallas kernels, prompt_attention(): pl.pallas_call(functools.partial(prompt_kernel, phase, carried), in_specs...  0.98 us
    pallas_call x1, Pallas kernels, base_product(): pl.pallas_call(functools.partial(base_kernel, offsets, slots), in_specs=[...  0.94 us
    pallas_call x1, Pallas kernels, finish(): pl.pallas_call(finish_kernel, in_specs=[VMEM] * 5, out_specs=VMEM, out_sh...  0.88 us
  transfers between devices with their start and end apart: 17, of which 4 were waited for; matrix products, arithmetic and copies ran while one was open for 0% of the time, Pallas kernels for 27%

profile of v2, /device:TPU:0, one launch (start us, length us, event | category | flops | bytes accessed | tf_op | source)
XLA Modules:
  0.0 41.7 jit_solution(6659673155888326241)
XLA Ops:
  0.6 3.0 %collective-permute-start = (bf16[16,8,128]{2,1,0:T(8,128)(2,1)}, bf16[16,8,128]{2,1,0:T(8,128)(2,1)S(1)}, u32[]{:S(2)}, u32[]{:S(2)}) collective-permute-start(bf16[16,8,128]{2,1,0:T(8,128)(2,1)} %refs_0_.1), channel_id=1, source_target_pairs={{0,1},{1,0},{2,3},{3,2},{4,5},{5,4},{6,7},{7,6},{8,9},{9,8},{10,11... | collective-permute-start | bytes 98312 | tf_op jit(solution)/shard_map/ppermute | solution.py:53
  3.7 1.5 %collective-permute-start.1 = (bf16[16,8,128]{2,1,0:T(8,128)(2,1)}, bf16[16,8,128]{2,1,0:T(8,128)(2,1)S(1)}, u32[]{:S(2)}, u32[]{:S(2)}) collective-permute-start(bf16[16,8,128]{2,1,0:T(8,128)(2,1)} %refs_0_.1), channel_id=1, source_target_pairs={{0,2},{1,3},{2,0},{3,1},{4,6},{5,7},{6,4},{7,5},{8,10},{9,11},{10,... | collective-permute-start | bytes 98312 | tf_op jit(solution)/shard_map/ppermute | solution.py:53
  5.2 0.0 collective-permute-start.2
  5.2 0.0 copy-start.1
  5.2 0.0 copy-start.4
  5.2 0.0 copy-start.5
  5.2 0.0 copy-start.2
  5.2 0.0 copy-start.3
  5.2 0.0 copy-start.6
  5.2 3.7 %cache_attention.1 = (bf16[128,128]{1,0:T(8,128)(2,1)S(1)}, f32[16,8,128]{2,1,0:T(8,128)S(1)}, f32[16,8,128]{2,1,0:T(8,128)S(1)}, bf16[256,4096]{1,0:T(8,128)(2,1)S(1)}) custom-call(s32[16]{0:T(128)} %pos_hbm.1, bf16[16,8,128]{2,1,0:T(8,128)(2,1)} %refs_0_.1, bf16[16,4,128]{2,1,0:T(4,128)(2,1)} %bitcast.16, bf16[16,1024,128]{2,1,0:T(8,128)(2,1)} %bitcast.14, ...), custom_call_target="tpu_custom_call" | custom-call | flops 10000000000 | bytes 4194304 | tf_op jit(solution)/shard_map/cache_attention/pallas_call | solution.py:163
  8.9 0.0 collective-permute-done.refs_1_
  8.9 0.0 collective-permute-done.1.refs_2_
  8.9 1.3 %collective-permute-done.2.refs_3_ = bf16[16,8,128]{2,1,0:T(8,128)(2,1)S(1)} collective-permute-done((bf16[16,8,128]{2,1,0:T(8,128)(2,1)}, bf16[16,8,128]{2,1,0:T(8,128)(2,1)S(1)}, u32[]{:S(2)}, u32[]{:S(2)}) %collective-permute-start.2) | collective-permute-done | bytes 32800 | tf_op jit(solution)/shard_map/ppermute | solution.py:53
  10.2 0.0 copy-done.1
  10.2 0.0 copy-done.4
  10.2 0.0 copy-done.5
  10.2 0.6 %make_table.1.refs_0_ = bf16[36,8,128]{2,1,0:T(8,128)(2,1)S(1)} custom-call(s32[4]{0:T(128)S(1)} %copy-done.4, s32[4]{0:T(128)S(1)} %copy-done.5, bf16[16,8,128]{2,1,0:T(8,128)(2,1)S(1)} %copy-done.1, bf16[16,8,128]{2,1,0:T(8,128)(2,1)S(1)} %collective-permute-done.refs_1_, bf16[16,8,128]{2,1,0:T(8,128)(2,1)S(1)} %collective-permute-done.1.refs_2_, ...), custom_call_target="tpu_custom_call" | custom-call | flops 100000000 | bytes 200000 | tf_op jit(solution)/shard_map/make_table/pallas_call | solution.py:319
  10.8 1.6 %collective-permute-start.3 = (bf16[36,8,128]{2,1,0:T(8,128)(2,1)S(1)}, bf16[36,8,128]{2,1,0:T(8,128)(2,1)S(1)}, u32[]{:S(2)}, u32[]{:S(2)}) collective-permute-start(bf16[36,8,128]{2,1,0:T(8,128)(2,1)S(1)} %make_table.1.refs_0_), channel_id=1, source_target_pairs={{0,4},{1,5},{2,6},{3,7},{4,0},{5,1},{6,2},{7,3},{8,12},{9,13},{10,... | collective-permute-start | bytes 221192 | tf_op jit(solution)/shard_map/ppermute | solution.py:53
  12.5 2.6 %collective-permute-start.4 = (bf16[36,8,128]{2,1,0:T(8,128)(2,1)S(1)}, bf16[36,8,128]{2,1,0:T(8,128)(2,1)S(1)}, u32[]{:S(2)}, u32[]{:S(2)}) collective-permute-start(bf16[36,8,128]{2,1,0:T(8,128)(2,1)S(1)} %make_table.1.refs_0_), channel_id=1, source_target_pairs={{0,8},{1,9},{2,10},{3,11},{4,12},{5,13},{6,14},{7,15},{8,0},{9,1},... | collective-permute-start | bytes 221192 | tf_op jit(solution)/shard_map/ppermute | solution.py:53
  15.1 0.2 collective-permute-start.5
  15.3 0.0 copy-done.2
  15.3 0.0 copy-done.3
  15.3 0.0 copy-done.6
  15.3 4.3 %project.1 = (bf16[2,256,128]{2,1,0:T(8,128)(2,1)S(1)}, bf16[2,256,128]{2,1,0:T(8,128)(2,1)S(1)}) custom-call(s32[4]{0:T(128)S(1)} %copy-done.3, bf16[256,4096]{1,0:T(8,128)(2,1)S(1)} %get-tuple-element.16.hid, f32[1,4096]{1,0:T(1,128)S(1)} %bitcast.11, f32[1,128]{1,0:T(1,128)S(1)} %copy-done.6, bf16[16384,128]{1,0:T(8,128)(2,1)} %bitcast.15), custom_call_target="tpu_custom_call" | custom-call | flops 10000000000 | bytes 6291456 | tf_op jit(solution)/shard_map/project/pallas_call | solution.py:259
  19.6 0.0 collective-permute-done.3.refs_1_
  19.6 0.0 collective-permute-done.4.refs_2_
  19.7 1.6 %collective-permute-done.5.refs_3_ = bf16[36,8,128]{2,1,0:T(8,128)(2,1)S(1)} collective-permute-done((bf16[36,8,128]{2,1,0:T(8,128)(2,1)S(1)}, bf16[36,8,128]{2,1,0:T(8,128)(2,1)S(1)}, u32[]{:S(2)}, u32[]{:S(2)}) %collective-permute-start.5) | collective-permute-done | bytes 73760 | tf_op jit(solution)/shard_map/ppermute | solution.py:53
  21.2 0.0 copy-start
  21.2 1.0 %prompt_attention.1 = (bf16[176,128]{1,0:T(8,128)(2,1)S(1)}, bf16[64,8,128]{2,1,0:T(8,128)(2,1)S(1)}) custom-call(s32[4]{0:T(128)S(1)} %copy-done.3, s32[4]{0:T(128)S(1)} %copy-done.4, s32[4]{0:T(128)S(1)} %copy-done.5, bf16[2,256,128]{2,1,0:T(8,128)(2,1)S(1)} %get-tuple-element.17.k_ref, bf16[2,256,128]{2,1,0:T(8,128)(2,1)S(1)} %get-tuple-element.18.v_ref, ...), custom_call_target="tpu_custom_call" | custom-call | flops 2000000000 | bytes 500000 | tf_op jit(solution)/shard_map/prompt_attention/pallas_call | solution.py:438
  22.2 0.8 %collective-permute-start.6 = (bf16[176,128]{1,0:T(8,128)(2,1)S(1)}, bf16[176,128]{1,0:T(8,128)(2,1)S(1)}, u32[]{:S(2)}, u32[]{:S(2)}) collective-permute-start(bf16[176,128]{1,0:T(8,128)(2,1)S(1)} %get-tuple-element.21.refs_0_), channel_id=1, source_target_pairs={{0,1},{1,0},{2,3},{3,2},{4,5},{5,4},{6,7},{7,6},{8,9},{9,8},{10,11... | collective-permute-start | bytes 135176 | tf_op jit(solution)/shard_map/ppermute | solution.py:53
  23.0 1.5 %collective-permute-start.7 = (bf16[176,128]{1,0:T(8,128)(2,1)S(1)}, bf16[176,128]{1,0:T(8,128)(2,1)S(1)}, u32[]{:S(2)}, u32[]{:S(2)}) collective-permute-start(bf16[176,128]{1,0:T(8,128)(2,1)S(1)} %get-tuple-element.21.refs_0_), channel_id=1, source_target_pairs={{0,2},{1,3},{2,0},{3,1},{4,6},{5,7},{6,4},{7,5},{8,10},{9,11},{10,... | collective-permute-start | bytes 135176 | tf_op jit(solution)/shard_map/ppermute | solution.py:53
  24.5 1.3 %collective-permute-start.8 = (bf16[176,128]{1,0:T(8,128)(2,1)S(1)}, bf16[176,128]{1,0:T(8,128)(2,1)S(1)}, u32[]{:S(2)}, u32[]{:S(2)}) collective-permute-start(bf16[176,128]{1,0:T(8,128)(2,1)S(1)} %get-tuple-element.21.refs_0_), channel_id=1, source_target_pairs={{0,3},{1,2},{2,1},{3,0},{4,7},{5,6},{6,5},{7,4},{8,11},{9,10},{10,... | collective-permute-start | bytes 135176 | tf_op jit(solution)/shard_map/ppermute | solution.py:53
  25.8 0.7 %collective-permute-start.12 = (bf16[512,128]{1,0:T(8,128)(2,1)S(1)}, bf16[512,128]{1,0:T(8,128)(2,1)S(1)}, u32[]{:S(2)}, u32[]{:S(2)}) collective-permute-start(bf16[512,128]{1,0:T(8,128)(2,1)S(1)} %bitcast.7), channel_id=1, source_target_pairs={{0,1},{1,0},{2,3},{3,2},{4,5},{5,4},{6,7},{7,6},{8,9},{9,8},{10,11... | collective-permute-start | bytes 393224 | tf_op jit(solution)/shard_map/ppermute | solution.py:53
  26.5 1.5 %collective-permute-start.13 = (bf16[512,128]{1,0:T(8,128)(2,1)S(1)}, bf16[512,128]{1,0:T(8,128)(2,1)S(1)}, u32[]{:S(2)}, u32[]{:S(2)}) collective-permute-start(bf16[512,128]{1,0:T(8,128)(2,1)S(1)} %bitcast.8), channel_id=1, source_target_pairs={{0,2},{1,3},{2,0},{3,1},{4,6},{5,7},{6,4},{7,5},{8,10},{9,11},{10,... | collective-permute-start | bytes 393224 | tf_op jit(solution)/shard_map/ppermute | solution.py:53
  28.0 0.0 collective-permute-done.6.refs_1_
  28.0 1.3 %collective-permute-start.14 = (bf16[512,128]{1,0:T(8,128)(2,1)S(1)}, bf16[512,128]{1,0:T(8,128)(2,1)S(1)}, u32[]{:S(2)}, u32[]{:S(2)}) collective-permute-start(bf16[512,128]{1,0:T(8,128)(2,1)S(1)} %bitcast.9), channel_id=1, source_target_pairs={{0,3},{1,2},{2,1},{3,0},{4,7},{5,6},{6,5},{7,4},{8,11},{9,10},{10,... | collective-permute-start | bytes 393224 | tf_op jit(solution)/shard_map/ppermute | solution.py:53
  29.3 0.0 collective-permute-done.7.refs_2_
  29.3 0.3 collective-permute-done.8.refs_3_
  29.5 0.4 merge_states.1.refs_0_
  29.9 0.1 collective-permute-start.9
  30.0 3.0 %collective-permute-start.10 = (bf16[176,128]{1,0:T(8,128)(2,1)S(1)}, bf16[176,128]{1,0:T(8,128)(2,1)S(1)}, u32[]{:S(2)}, u32[]{:S(2)}) collective-permute-start(bf16[176,128]{1,0:T(8,128)(2,1)S(1)} %merge_states.1.refs_0_), channel_id=1, source_target_pairs={{0,8},{1,9},{2,10},{3,11},{4,12},{5,13},{6,14},{7,15},{8,0},{9,1},... | collective-permute-start | bytes 135176 | tf_op jit(solution)/shard_map/ppermute | solution.py:53
  33.0 0.0 collective-permute-done.12.refs_1_
  33.0 1.4 %collective-permute-start.11 = (bf16[176,128]{1,0:T(8,128)(2,1)S(1)}, bf16[176,128]{1,0:T(8,128)(2,1)S(1)}, u32[]{:S(2)}, u32[]{:S(2)}) collective-permute-start(bf16[176,128]{1,0:T(8,128)(2,1)S(1)} %merge_states.1.refs_0_), channel_id=1, source_target_pairs={{0,12},{1,13},{2,14},{3,15},{4,8},{5,9},{6,10},{7,11},{8,4},{9,5},... | collective-permute-start | bytes 135176 | tf_op jit(solution)/shard_map/ppermute | solution.py:53
  34.4 0.0 collective-permute-done.13.refs_2_
  34.4 0.0 collective-permute-done.14.refs_3_
  34.4 0.0 copy-done
  34.4 0.9 %base_product.1 = (f32[128,256]{1,0:T(8,128)S(1)}, f32[128,256]{1,0:T(8,128)S(1)}, f32[128,24]{1,0:T(8,128)S(1)}) custom-call(s32[4]{0:T(128)S(1)} %copy-done.4, s32[4]{0:T(128)S(1)} %copy-done.5, bf16[8,128,256]{2,1,0:T(8,128)(2,1)S(1)} %copy-done, bf16[512,128]{1,0:T(8,128)(2,1)S(1)} %bitcast.10, bf16[512,128]{1,0:T(8,128)(2,1)S(1)} %collective-permute-done.12.refs_1_, ...), custom_call_target="tpu_custom_call" | custom-call | flops 2000000000 | bytes 1000000 | tf_op jit(solution)/shard_map/base_product/pallas_call | solution.py:504
  35.4 0.1 collective-permute-start.15
  35.4 0.0 collective-permute-done.9.refs_1_
  35.4 0.0 collective-permute-done.10.refs_2_
  35.5 3.4 %collective-permute-done.11.refs_3_ = bf16[176,128]{1,0:T(8,128)(2,1)S(1)} collective-permute-done((bf16[176,128]{1,0:T(8,128)(2,1)S(1)}, bf16[176,128]{1,0:T(8,128)(2,1)S(1)}, u32[]{:S(2)}, u32[]{:S(2)}) %collective-permute-start.11) | collective-permute-done | bytes 45088 | tf_op jit(solution)/shard_map/ppermute | solution.py:53
  38.9 0.5 %answer_product.1 = (bf16[160,128]{1,0:T(8,128)(2,1)S(1)}, f32[24,256]{1,0:T(8,128)S(1)}) custom-call(bf16[8,128,256]{2,1,0:T(8,128)(2,1)S(1)} %copy-done, bf16[176,128]{1,0:T(8,128)(2,1)S(1)} %merge_states.1.refs_0_, bf16[176,128]{1,0:T(8,128)(2,1)S(1)} %collective-permute-done.9.refs_1_, bf16[176,128]{1,0:T(8,128)(2,1)S(1)} %collective-permute-done.10.refs_2_, ...), custom_call_target="tpu_custom_call" | custom-call | flops 1000000000 | bytes 1000000 | tf_op jit(solution)/shard_map/answer_product/pallas_call | solution.py:535
  39.4 0.0 collective-permute-start.16
  39.4 1.4 %attended_rows.1 = bf16[16,8,128]{2,1,0:T(8,128)(2,1)} custom-call(s32[4]{0:T(128)S(1)} %copy-done.4, s32[4]{0:T(128)S(1)} %copy-done.5, f32[16,8,128]{2,1,0:T(8,128)S(1)} %get-tuple-element.15.o_ref, bf16[20,8,128]{2,1,0:T(8,128)(2,1)S(1)} %bitcast.12), custom_call_target="tpu_custom_call" | custom-call | flops 500000000 | bytes 1000000 | tf_op jit(solution)/shard_map/attended_rows/pallas_call | solution.py:563
  40.8 0.0 collective-permute-done.16.part_taken
  40.8 0.0 collective-permute-done.15.taken
  40.8 0.9 %finish.1 = bf16[128,256]{1,0:T(8,128)(2,1)} custom-call(f32[128,256]{1,0:T(8,128)S(1)} %get-tuple-element.24.keep, f32[128,256]{1,0:T(8,128)S(1)} %collective-permute-done.15.taken, f32[24,256]{1,0:T(8,128)S(1)} %get-tuple-element.26.part, f32[24,256]{1,0:T(8,128)S(1)} %collective-permute-done.16.part_taken, f32[128,24]{1,0:T(8,128)S(1)} %get-tuple-element.27.pick), custom_call_target="tpu_custom_call" | custom-call | tf_op jit(solution)/shard_map/finish/pallas_call | solution.py:585
Async XLA Ops:
  0.6 8.3 %collective-permute-start = (bf16[16,8,128]{2,1,0:T(8,128)(2,1)}, bf16[16,8,128]{2,1,0:T(8,128)(2,1)S(1)}, u32[]{:S(2)}, u32[]{:S(2)}) collective-permute-start(bf16[16,8,128]{2,1,0:T(8,128)(2,1)} %refs_0_.1), channel_id=1, source_target_pairs={{0,1},{1,0},{2,3},{3,2},{4,5},{5,4},{6,7},{7,6},{8,9},{9,8},{10,11... | collective-permute-start | bytes 98312 | tf_op jit(solution)/shard_map/ppermute | solution.py:53
  3.7 5.3 %collective-permute-start.1 = (bf16[16,8,128]{2,1,0:T(8,128)(2,1)}, bf16[16,8,128]{2,1,0:T(8,128)(2,1)S(1)}, u32[]{:S(2)}, u32[]{:S(2)}) collective-permute-start(bf16[16,8,128]{2,1,0:T(8,128)(2,1)} %refs_0_.1), channel_id=1, source_target_pairs={{0,2},{1,3},{2,0},{3,1},{4,6},{5,7},{6,4},{7,5},{8,10},{9,11},{10,... | collective-permute-start | bytes 98312 | tf_op jit(solution)/shard_map/ppermute | solution.py:53
  5.2 5.0 %collective-permute-start.2 = (bf16[16,8,128]{2,1,0:T(8,128)(2,1)}, bf16[16,8,128]{2,1,0:T(8,128)(2,1)S(1)}, u32[]{:S(2)}, u32[]{:S(2)}) collective-permute-start(bf16[16,8,128]{2,1,0:T(8,128)(2,1)} %refs_0_.1), channel_id=1, source_target_pairs={{0,3},{1,2},{2,1},{3,0},{4,7},{5,6},{6,5},{7,4},{8,11},{9,10},{10,... | collective-permute-start | bytes 98312 | tf_op jit(solution)/shard_map/ppermute | solution.py:53
  5.2 5.0 %copy-start.1 = (bf16[16,8,128]{2,1,0:T(8,128)(2,1)S(1)}, bf16[16,8,128]{2,1,0:T(8,128)(2,1)}, u32[]{:S(2)}) copy-start(bf16[16,8,128]{2,1,0:T(8,128)(2,1)} %refs_0_.1) | copy-start | bytes 98308
  5.2 5.0 %copy-start.4 = (s32[4]{0:T(128)S(1)}, s32[4]{0:T(128)}, u32[]{:S(2)}) copy-start(s32[4]{0:T(128)} %owner.7) | copy-start | bytes 52
  5.2 5.0 %copy-start.5 = (s32[4]{0:T(128)S(1)}, s32[4]{0:T(128)}, u32[]{:S(2)}) copy-start(s32[4]{0:T(128)} %counts.7) | copy-start | bytes 52
  5.2 10.1 %copy-start.2 = (f32[4096]{0:T(1024)S(1)}, f32[4096]{0:T(1024)}, u32[]{:S(2)}) copy-start(f32[4096]{0:T(1024)} %param.13) | copy-start | bytes 49156
  5.2 10.1 %copy-start.3 = (s32[4]{0:T(128)S(1)}, s32[4]{0:T(128)}, u32[]{:S(2)}) copy-start(s32[4]{0:T(128)} %excess.3) | copy-start | bytes 52
  5.2 10.1 %copy-start.6 = (f32[1,128]{1,0:T(1,128)S(1)}, f32[1,128]{1,0:T(1,128)}, u32[]{:S(2)}) copy-start(f32[1,128]{1,0:T(1,128)} %constant.2.clone.freq_ref) | copy-start | bytes 1540
  10.8 8.8 %collective-permute-start.3 = (bf16[36,8,128]{2,1,0:T(8,128)(2,1)S(1)}, bf16[36,8,128]{2,1,0:T(8,128)(2,1)S(1)}, u32[]{:S(2)}, u32[]{:S(2)}) collective-permute-start(bf16[36,8,128]{2,1,0:T(8,128)(2,1)S(1)} %make_table.1.refs_0_), channel_id=1, source_target_pairs={{0,4},{1,5},{2,6},{3,7},{4,0},{5,1},{6,2},{7,3},{8,12},{9,13},{10,... | collective-permute-start | bytes 221192 | tf_op jit(solution)/shard_map/ppermute | solution.py:53
  12.5 7.2 %collective-permute-start.4 = (bf16[36,8,128]{2,1,0:T(8,128)(2,1)S(1)}, bf16[36,8,128]{2,1,0:T(8,128)(2,1)S(1)}, u32[]{:S(2)}, u32[]{:S(2)}) collective-permute-start(bf16[36,8,128]{2,1,0:T(8,128)(2,1)S(1)} %make_table.1.refs_0_), channel_id=1, source_target_pairs={{0,8},{1,9},{2,10},{3,11},{4,12},{5,13},{6,14},{7,15},{8,0},{9,1},... | collective-permute-start | bytes 221192 | tf_op jit(solution)/shard_map/ppermute | solution.py:53
  15.1 6.2 %collective-permute-start.5 = (bf16[36,8,128]{2,1,0:T(8,128)(2,1)S(1)}, bf16[36,8,128]{2,1,0:T(8,128)(2,1)S(1)}, u32[]{:S(2)}, u32[]{:S(2)}) collective-permute-start(bf16[36,8,128]{2,1,0:T(8,128)(2,1)S(1)} %make_table.1.refs_0_), channel_id=1, source_target_pairs={{0,12},{1,13},{2,14},{3,15},{4,8},{5,9},{6,10},{7,11},{8,4},{9,5},... | collective-permute-start | bytes 221192 | tf_op jit(solution)/shard_map/ppermute | solution.py:53
  21.2 13.2 %copy-start = (bf16[8,128,256]{2,1,0:T(8,128)(2,1)S(1)}, bf16[8,128,256]{2,1,0:T(8,128)(2,1)}, u32[]{:S(2)}) copy-start(bf16[8,128,256]{2,1,0:T(8,128)(2,1)} %w_ref.3) | copy-start | bytes 1572868
  22.2 5.8 %collective-permute-start.6 = (bf16[176,128]{1,0:T(8,128)(2,1)S(1)}, bf16[176,128]{1,0:T(8,128)(2,1)S(1)}, u32[]{:S(2)}, u32[]{:S(2)}) collective-permute-start(bf16[176,128]{1,0:T(8,128)(2,1)S(1)} %get-tuple-element.21.refs_0_), channel_id=1, source_target_pairs={{0,1},{1,0},{2,3},{3,2},{4,5},{5,4},{6,7},{7,6},{8,9},{9,8},{10,11... | collective-permute-start | bytes 135176 | tf_op jit(solution)/shard_map/ppermute | solution.py:53
  23.0 6.3 %collective-permute-start.7 = (bf16[176,128]{1,0:T(8,128)(2,1)S(1)}, bf16[176,128]{1,0:T(8,128)(2,1)S(1)}, u32[]{:S(2)}, u32[]{:S(2)}) collective-permute-start(bf16[176,128]{1,0:T(8,128)(2,1)S(1)} %get-tuple-element.21.refs_0_), channel_id=1, source_target_pairs={{0,2},{1,3},{2,0},{3,1},{4,6},{5,7},{6,4},{7,5},{8,10},{9,11},{10,... | collective-permute-start | bytes 135176 | tf_op jit(solution)/shard_map/ppermute | solution.py:53
  24.5 5.0 %collective-permute-start.8 = (bf16[176,128]{1,0:T(8,128)(2,1)S(1)}, bf16[176,128]{1,0:T(8,128)(2,1)S(1)}, u32[]{:S(2)}, u32[]{:S(2)}) collective-permute-start(bf16[176,128]{1,0:T(8,128)(2,1)S(1)} %get-tuple-element.21.refs_0_), channel_id=1, source_target_pairs={{0,3},{1,2},{2,1},{3,0},{4,7},{5,6},{6,5},{7,4},{8,11},{9,10},{10,... | collective-permute-start | bytes 135176 | tf_op jit(solution)/shard_map/ppermute | solution.py:53
  25.8 7.3 %collective-permute-start.12 = (bf16[512,128]{1,0:T(8,128)(2,1)S(1)}, bf16[512,128]{1,0:T(8,128)(2,1)S(1)}, u32[]{:S(2)}, u32[]{:S(2)}) collective-permute-start(bf16[512,128]{1,0:T(8,128)(2,1)S(1)} %bitcast.7), channel_id=1, source_target_pairs={{0,1},{1,0},{2,3},{3,2},{4,5},{5,4},{6,7},{7,6},{8,9},{9,8},{10,11... | collective-permute-start | bytes 393224 | tf_op jit(solution)/shard_map/ppermute | solution.py:53
  26.5 7.9 %collective-permute-start.13 = (bf16[512,128]{1,0:T(8,128)(2,1)S(1)}, bf16[512,128]{1,0:T(8,128)(2,1)S(1)}, u32[]{:S(2)}, u32[]{:S(2)}) collective-permute-start(bf16[512,128]{1,0:T(8,128)(2,1)S(1)} %bitcast.8), channel_id=1, source_target_pairs={{0,2},{1,3},{2,0},{3,1},{4,6},{5,7},{6,4},{7,5},{8,10},{9,11},{10,... | collective-permute-start | bytes 393224 | tf_op jit(solution)/shard_map/ppermute | solution.py:53
  28.0 6.4 %collective-permute-start.14 = (bf16[512,128]{1,0:T(8,128)(2,1)S(1)}, bf16[512,128]{1,0:T(8,128)(2,1)S(1)}, u32[]{:S(2)}, u32[]{:S(2)}) collective-permute-start(bf16[512,128]{1,0:T(8,128)(2,1)S(1)} %bitcast.9), channel_id=1, source_target_pairs={{0,3},{1,2},{2,1},{3,0},{4,7},{5,6},{6,5},{7,4},{8,11},{9,10},{10,... | collective-permute-start | bytes 393224 | tf_op jit(solution)/shard_map/ppermute | solution.py:53
  29.9 5.5 %collective-permute-start.9 = (bf16[176,128]{1,0:T(8,128)(2,1)S(1)}, bf16[176,128]{1,0:T(8,128)(2,1)S(1)}, u32[]{:S(2)}, u32[]{:S(2)}) collective-permute-start(bf16[176,128]{1,0:T(8,128)(2,1)S(1)} %merge_states.1.refs_0_), channel_id=1, source_target_pairs={{0,4},{1,5},{2,6},{3,7},{4,0},{5,1},{6,2},{7,3},{8,12},{9,13},{10,... | collective-permute-start | bytes 135176 | tf_op jit(solution)/shard_map/ppermute | solution.py:53
  30.0 5.4 %collective-permute-start.10 = (bf16[176,128]{1,0:T(8,128)(2,1)S(1)}, bf16[176,128]{1,0:T(8,128)(2,1)S(1)}, u32[]{:S(2)}, u32[]{:S(2)}) collective-permute-start(bf16[176,128]{1,0:T(8,128)(2,1)S(1)} %merge_states.1.refs_0_), channel_id=1, source_target_pairs={{0,8},{1,9},{2,10},{3,11},{4,12},{5,13},{6,14},{7,15},{8,0},{9,1},... | collective-permute-start | bytes 135176 | tf_op jit(solution)/shard_map/ppermute | solution.py:53
  33.0 5.8 %collective-permute-start.11 = (bf16[176,128]{1,0:T(8,128)(2,1)S(1)}, bf16[176,128]{1,0:T(8,128)(2,1)S(1)}, u32[]{:S(2)}, u32[]{:S(2)}) collective-permute-start(bf16[176,128]{1,0:T(8,128)(2,1)S(1)} %merge_states.1.refs_0_), channel_id=1, source_target_pairs={{0,12},{1,13},{2,14},{3,15},{4,8},{5,9},{6,10},{7,11},{8,4},{9,5},... | collective-permute-start | bytes 135176 | tf_op jit(solution)/shard_map/ppermute | solution.py:53
  35.4 5.4 %collective-permute-start.15 = (f32[128,256]{1,0:T(8,128)S(1)}, f32[128,256]{1,0:T(8,128)S(1)}, u32[]{:S(2)}, u32[]{:S(2)}) collective-permute-start(f32[128,256]{1,0:T(8,128)S(1)} %get-tuple-element.25), channel_id=1, source_target_pairs={{0,16},{16,0},{1,17},{17,1},{2,18},{18,2},{3,19},{19,3},{4,20},{20... | collective-permute-start | bytes 393224 | tf_op jit(solution)/shard_map/ppermute | solution.py:596
  39.4 1.4 %collective-permute-start.16 = (f32[24,256]{1,0:T(8,128)S(1)}, f32[24,256]{1,0:T(8,128)S(1)}, u32[]{:S(2)}, u32[]{:S(2)}) collective-permute-start(f32[24,256]{1,0:T(8,128)S(1)} %get-tuple-element.26.part), channel_id=1, source_target_pairs={{0,16},{16,0},{1,17},{17,1},{2,18},{18,2},{3,19},{19,3},{4,20},{20... | collective-permute-start | bytes 73736 | tf_op jit(solution)/shard_map/ppermute | solution.py:596
